TPU v7x, 256 devices: a whole 4x4x8 slice. The times are simulated.
256 devices in a mesh: chain: 16 (over z, core), dp: 16 (over y, x).
Axes of the slice: x: 4, y: 4, z: 8, core: 2. Of those that a mesh axis runs over, the one named last changes fastest.
Arguments:
- images_in: float32 [16, 1024, 1024], P('chain', 'dp'), may hold values from -8 to 8
- images_mid: float32 [16, 1024, 1024], P('chain', 'dp'), may hold values from -8 to 8
- images_out: float32 [16, 1024, 1000], P('chain', 'dp'), may hold values from -8 to 8
- ends_in: float32 [2, 1024, 1024], P(None, 'dp'), may hold values from -8 to 8
- ends_mid: float32 [2, 1024, 1024], P(None, 'dp'), may hold values from -8 to 8
- ends_out: float32 [2, 1024, 1000], P(None, 'dp'), may hold values from -8 to 8
- data_pool: bfloat16 [28672, 1024], P('dp'), may hold values from -6 to 6
- batch_rows: int32 [16, 14336], P('chain', 'dp'), may hold values from 0 to 1791
- labels: int32 [16, 14336], P('chain', 'dp'), may hold values from 0 to 999
- climbing: int32 [16], P('chain'), may hold values 0 or 1
Outputs:
- new_in: float32 [16, 1024, 1024], P('chain', 'dp')
- new_mid: float32 [16, 1024, 1024], P('chain', 'dp')
- new_out: float32 [16, 1024, 1000], P('chain', 'dp')
- energies: float32 [16], P('chain')
- arc_share: float32 [16], P('chain')
- bend: float32 [16], P('chain')
Inputs may be any that keep to these rules, and one draw needn't show every extreme that they name: batch_rows[i, b] names a row of the pool shard held by dp index b // 896.
All inputs are finite; a program needn't handle non-finite values. No bound on the sum of `climbing` on one device may be relied on, other than what follows from the above.
Results may differ from a plain program's by a relative error of at most 0.0023.
Values may be sent and summed in bfloat16 or wider, within the bound.
A program may use at most 128 MiB of HBM per device.

v0:
```python
import jax
import jax.numpy as jnp
from jax import lax
from jax.sharding import Mesh
from jax.sharding import PartitionSpec as P

DP = ("dp_0", "dp_1")


SPRING = 0.03
EPS = 1e-06


def for_sending(value):

    def short(part):
        return part.astype(jnp.bfloat16) if part.dtype == jnp.float32 else part

    return jax.tree.map(short, value)


def gather_axes(value, axes, dim):
    if not axes:
        return value
    nearer = lax.all_gather(value, axes[-1], axis=dim, tiled=True)
    return gather_axes(nearer, axes[:-1], dim)


def in_one_piece(arrays, axis, dim, along):
    both = jnp.concatenate(arrays, axis=along)
    whole, at, gathered = (lax.psum_scatter(both, axis, scatter_dimension=dim, tiled=True), 0, [])
    for a in arrays:
        gathered.append(lax.slice_in_dim(whole, at, at + a.shape[along], axis=along))
        at += a.shape[along]
    return tuple(gathered)


def passed_along(block, axis, distance):
    devices = range(lax.axis_size(axis))
    route = [(i - distance, i) for i in devices if i - distance in devices]
    return lax.ppermute(block, axis, route)


def over_axes(value, axes):
    for axis in axes:
        value = lax.psum(value, axis)
    return value


def joined_along(blocks, dim):
    blocks = jnp.moveaxis(blocks, 0, dim)
    dims = blocks.shape
    return blocks.reshape(*dims[:dim], dims[dim] * dims[dim + 1], *dims[dim + 2 :])


def copy_for_each(value, axis):
    peers = lax.axis_size(axis)
    return lax.all_to_all(
        jnp.broadcast_to(value[None], (peers, *value.shape)), axis, 0, 0, tiled=True
    )


def gathered_copies(value, axis, dim):
    return joined_along(copy_for_each(value, axis), dim)


def silu_slope(pre):
    sig = jax.nn.sigmoid(pre)
    return sig * (1.0 + pre * (1.0 - sig))


def dot_nt(left, right):
    return lax.dot_general(
        left, right, (((1,), (1,)), ((), ())), preferred_element_type=jnp.float32
    )


def dot_tn(left, right):
    return lax.dot_general(
        left, right, (((0,), (0,)), ((), ())), preferred_element_type=jnp.float32
    )


def inner(first, second):
    total = jnp.float32(0.0)
    for left, right in zip(first, second):
        total = total + jnp.sum(left * right)
    return total


def on_device(
    images_in,
    images_mid,
    images_out,
    ends_in,
    ends_mid,
    ends_out,
    data_pool,
    batch_rows,
    labels,
    climbing,
):
    own = (images_in[0], images_mid[0], images_out[0])
    width = data_pool.shape[1]
    hidden_units = images_in.shape[2]
    classes = images_out.shape[2]
    groups = lax.axis_size(DP)
    factors = (width ** (-0.5), hidden_units ** (-0.5), width ** (-0.5))
    lowered = tuple(((p * f).astype(jnp.bfloat16) for p, f in zip(own, factors)))
    w_in, w_mid, w_out = jax.tree.map(
        lambda part, own: part.astype(own.dtype),
        jax.tree.map(lambda part: gather_axes(part, DP, 0), for_sending(lowered)),
        lowered,
    )
    rows = data_pool[batch_rows[0]]
    batch = rows.shape[0] * groups
    pre = jnp.dot(rows, w_in, preferred_element_type=jnp.float32)
    hid = jax.nn.silu(pre).astype(jnp.bfloat16)
    resid = (
        rows.astype(jnp.float32) + jnp.dot(hid, w_mid, preferred_element_type=jnp.float32)
    ).astype(jnp.bfloat16)
    logits = jnp.dot(resid, w_out, preferred_element_type=jnp.float32)
    target = (labels[0][:, None] == jnp.arange(classes, dtype=jnp.int32)[None, :]).astype(
        jnp.float32
    )
    err = logits - target
    norm = 1.0 / (batch * classes)
    energy_part = 0.5 * norm * jnp.sum(err * err)
    d_logits = (err * norm).astype(jnp.bfloat16)
    d_resid = dot_nt(d_logits, w_out).astype(jnp.bfloat16)
    d_pre = (dot_nt(d_resid, w_mid) * silu_slope(pre)).astype(jnp.bfloat16)
    summed = tuple(
        (
            part.astype(jnp.float32)
            for part in in_one_piece(
                (
                    dot_tn(rows, d_pre).astype(jnp.bfloat16),
                    dot_tn(hid, d_resid).astype(jnp.bfloat16),
                    dot_tn(resid, d_logits).astype(jnp.bfloat16),
                ),
                DP,
                0,
                1,
            )
        )
    )
    grads = tuple((g * f for g, f in zip(summed, factors)))
    index = lax.axis_index("chain")
    count = lax.axis_size("chain")
    ends = (ends_in, ends_mid, ends_out)
    left = (
        passed_along(own[0].astype(jnp.bfloat16), "chain", 1).astype(jnp.float32),
        passed_along(own[1].astype(jnp.bfloat16), "chain", 1).astype(jnp.float32),
        passed_along(own[2].astype(jnp.bfloat16), "chain", 1).astype(jnp.float32),
    )
    right = (
        passed_along(own[0].astype(jnp.bfloat16), "chain", -1).astype(jnp.float32),
        passed_along(own[1].astype(jnp.bfloat16), "chain", -1).astype(jnp.float32),
        passed_along(own[2].astype(jnp.bfloat16), "chain", -1).astype(jnp.float32),
    )
    left = tuple((jnp.where(index == 0, e[0], piece) for e, piece in zip(ends, left)))
    right = tuple((jnp.where(index == count - 1, e[1], piece) for e, piece in zip(ends, right)))
    ahead = tuple((r - o for r, o in zip(right, own)))
    behind = tuple((o - l for o, l in zip(own, left)))
    sq_ahead, sq_behind, cross, g_ahead, g_behind, g_g, energy = (
        over_axes(inner(ahead, ahead), DP),
        over_axes(inner(behind, behind), DP),
        over_axes(inner(ahead, behind), DP),
        over_axes(inner(grads, ahead), DP),
        over_axes(inner(grads, behind), DP),
        over_axes(inner(grads, grads), DP),
        over_axes(energy_part, DP),
    )
    len_ahead = jnp.sqrt(sq_ahead + EPS)
    len_behind = jnp.sqrt(sq_behind + EPS)
    raw_sq = (
        sq_ahead / (len_ahead * len_ahead)
        + sq_behind / (len_behind * len_behind)
        + 2.0 * cross / (len_ahead * len_behind)
    )
    raw_len = jnp.sqrt(raw_sq + EPS)
    tau = tuple(((a / len_ahead + b / len_behind) / raw_len for a, b in zip(ahead, behind)))
    along = (g_ahead / len_ahead + g_behind / len_behind) / raw_len
    tau_sq = raw_sq / (raw_sq + EPS)
    pair = jnp.stack([len_behind, len_ahead])[None, :]
    table = gathered_copies(pair, "chain", 0)
    order = jnp.arange(table.shape[0], dtype=jnp.int32)
    arc = jnp.sum(jnp.where(order <= index, table[:, 0], 0.0))
    band = jnp.sum(table[:, 0]) + table[-1, 1]
    goal = (index + 1).astype(jnp.float32) / (count + 1) * band
    coef = jnp.where(climbing[0] == 1, 2.0 * along, along + SPRING * (goal - arc) / band)
    force = tuple((-g + coef * t for g, t in zip(grads, tau)))
    force_sq = g_g - 2.0 * coef * along + coef * coef * tau_sq
    scale = band / (count + 1) / jnp.sqrt(force_sq + EPS)
    new = tuple(((o + scale * f)[None] for o, f in zip(own, force)))
    return (new[0], new[1], new[2], energy[None], (arc / band)[None], (0.5 * raw_len)[None])


def solution(mesh):
    torus = Mesh(mesh.devices.reshape(mesh.shape["chain"], 4, 4), ("chain", "dp_0", "dp_1"))
    in_specs = (
        P("chain", DP, None),
        P("chain", DP, None),
        P("chain", DP, None),
        P(None, DP, None),
        P(None, DP, None),
        P(None, DP, None),
        P(DP, None),
        P("chain", DP),
        P("chain", DP),
        P("chain"),
    )
    out_specs = (
        P("chain", DP, None),
        P("chain", DP, None),
        P("chain", DP, None),
        P("chain"),
        P("chain"),
        P("chain"),
    )
    return jax.shard_map(
        on_device, mesh=torus, in_specs=in_specs, out_specs=out_specs, check_vma=False
    )
```

profile of v0, /device:TPU:2, one launch (start us, length us, event | category | flops | bytes accessed | tf_op | source)
XLA Modules:
  0.0 325.2 jit_solution(15012936727917754198)
XLA Ops:
  7.2 1.0 fusion.10
  8.2 14.3 %all_gather.18 = bf16[256,1024]{1,0:T(8,128)(2,1)} all-gather(bf16[64,1024]{1,0:T(8,128)(2,1)S(1)} %fusion.10), channel_id=1, replica_groups=mesh['chain'=16,'dp_0'=4,'dp_1'=4] {'dp_1'}, dimensions={0}, use_global_device_ids=true | all-gather | bytes 655360 | tf_op jit(solution)/shard_map/all_gather | solution.py:25
  23.5 13.9 %all_gather.20 = bf16[256,1024]{1,0:T(8,128)(2,1)} all-gather(bf16[64,1024]{1,0:T(8,128)(2,1)S(1)} %fusion.7), channel_id=1, replica_groups=mesh['chain'=16,'dp_0'=4,'dp_1'=4] {'dp_1'}, dimensions={0}, use_global_device_ids=true | all-gather | bytes 655360 | tf_op jit(solution)/shard_map/all_gather | solution.py:25
  37.5 1.0 fusion.4
  38.5 13.5 %all_gather.22 = bf16[256,1000]{1,0:T(8,128)(2,1)} all-gather(bf16[64,1000]{1,0:T(8,128)(2,1)S(1)} %fusion.4), channel_id=1, replica_groups=mesh['chain'=16,'dp_0'=4,'dp_1'=4] {'dp_1'}, dimensions={0}, use_global_device_ids=true | all-gather | bytes 640000 | tf_op jit(solution)/shard_map/all_gather | solution.py:25
  52.2 7.7 %gather_fusion = bf16[896,1024]{1,0:T(8,128)(2,1)S(1)} fusion(bf16[1792,1024]{1,0:T(8,128)(2,1)} %param.16, s32[1024]{0:T(1024)S(1)} %pad_clamp_fusion), kind=kCustom, calls=%fused_computation | custom fusion | bytes 3673600 | tf_op jit(solution)/shard_map/gather | solution.py:115
  60.0 6.1 %fusion.23 = f32[896,1024]{1,0:T(8,128)} fusion(bf16[896,1024]{1,0:T(8,128)(2,1)S(1)} %gather_fusion, bf16[1024,1024]{1,0:T(8,128)(2,1)} %all-gather.4.cloned.1.call-done), kind=kOutput, calls=%fused_computation.72 | convolution fusion | flops 1879048192 | bytes 7602176 | tf_op jit(solution)/shard_map/dot_general | solution.py:117
  66.0 27.8 %all-gather.6.cloned.1.call-done = bf16[1024,1024]{1,0:T(8,128)(2,1)} async-done(((bf16[256,1024]{1,0:T(8,128)(2,1)}), bf16[1024,1024]{1,0:T(8,128)(2,1)}) %all-gather.6.cloned.1.call-update) | async-done | bytes 2097168 | tf_op jit(solution)/shard_map/all_gather | solution.py:25
  93.8 6.2 %add_convert_fusion = bf16[896,1024]{1,0:T(8,128)(2,1)} fusion(bf16[896,1024]{1,0:T(8,128)(2,1)S(1)} %gather_fusion, bf16[1024,1024]{1,0:T(8,128)(2,1)} %all-gather.6.cloned.1.call-done, f32[896,1024]{1,0:T(8,128)} %fusion.23), kind=kOutput, calls=%fused_computation.3 | convolution fusion | flops 1886388224 | bytes 9437184 | tf_op jit(solution)/shard_map/dot_general | solution.py:120
  100.0 29.1 %all-gather.8.cloned.1.call-done = bf16[1024,1000]{1,0:T(8,128)(2,1)} async-done(((bf16[256,1000]{1,0:T(8,128)(2,1)}), bf16[1024,1000]{1,0:T(8,128)(2,1)}) %all-gather.8.cloned.1.call-update) | async-done | bytes 2048016 | tf_op jit(solution)/shard_map/all_gather | solution.py:25
  129.1 5.6 %multiply_reduce_fusion = (f32[]{:T(128)}, f32[896,1000]{0,1:T(8,128)S(1)}) fusion(s32[896]{0:T(1024)S(1)} %reduce.2, bf16[896,1024]{1,0:T(8,128)(2,1)} %add_convert_fusion, bf16[1024,1000]{1,0:T(8,128)(2,1)} %all-gather.8.cloned.1.call-done), kind=kOutput, calls=%fused_computation.6 | convolution fusion | flops 1839488000 | bytes 7470596 | tf_op jit(solution)/shard_map/dot_general | solution.py:122
  134.7 3.6 %convolution_convert_fusion.2 = bf16[1024,1000]{0,1:T(8,128)(2,1)} fusion(bf16[896,1024]{1,0:T(8,128)(2,1)S(1)} %copy-done.13, f32[896,1000]{0,1:T(8,128)S(1)} %get-tuple-element.59, s32[896]{0:T(1024)S(1)} %reduce.2), kind=kOutput, calls=%fused_computation.12 | convolution fusion | flops 1840512000 | bytes 7470592 | tf_op jit(solution)/shard_map/dot_general | solution.py:79
  138.3 2.1 convolution_convert_fusion.3
  140.4 1.2 copy-done.14
  141.7 2.7 convolution_convert_fusion
  144.4 9.9 %convolution_convert_fusion.1 = bf16[1024,1024]{0,1:T(8,128)(2,1)} fusion(bf16[896,1024]{1,0:T(8,128)(2,1)} %copy-done.3, f32[896,1024]{1,0:T(8,128)} %fusion.23, bf16[896,1024]{1,0:T(8,128)(2,1)} %copy-done.14, bf16[1024,1024]{1,0:T(8,128)(2,1)} %all-gather.6.cloned.1.call-done), kind=kOutput, calls=%fused_computation.11 | convolution fusion | flops 3767402496 | bytes 11534336 | tf_op jit(solution)/shard_map/dot_general | solution.py:79
  154.3 5.5 %pad_maximum_fusion = bf16[1024,3048]{0,1:T(8,128)(2,1)} fusion(bf16[1024,1000]{0,1:T(8,128)(2,1)} %convolution_convert_fusion.2, bf16[1024,1024]{0,1:T(8,128)(2,1)S(1)} %convolution_convert_fusion, bf16[1024,1024]{0,1:T(8,128)(2,1)} %convolution_convert_fusion.1), kind=kLoop, calls=%fused_computation.1 | loop fusion | flops 18726912 | bytes 12484608 | tf_op jit(solution)/shard_map/concatenate | solution.py:30
  159.8 8.8 %copy.44 = bf16[1024,3048]{1,0:T(8,128)(2,1)} copy(bf16[1024,3048]{0,1:T(8,128)(2,1)} %pad_maximum_fusion) | data formatting | bytes 12484608
  169.6 1.7 collective-permute-start
  171.3 1.3 collective-permute-start.3
  172.6 4.5 %collective-permute-start.1 = (bf16[64,1024]{1,0:T(8,128)(2,1)S(1)}, bf16[64,1024]{1,0:T(8,128)(2,1)S(1)}, u32[]{:S(2)}, u32[]{:S(2)}) collective-permute-start(bf16[64,1024]{1,0:T(8,128)(2,1)S(1)} %bitcast_convert_fusion.1), channel_id=1, source_target_pairs={{0,16},{16,32},{32,48},{48,64},{64,80},{80,96},{96,112},{112,128},... | collective-permute-start | bytes 393224 | tf_op jit(solution)/shard_map/ppermute | solution.py:41
  177.2 1.3 collective-permute-start.4
  179.2 4.9 %collective-permute-start.2 = (bf16[64,1000]{1,0:T(8,128)(2,1)}, bf16[64,1000]{1,0:T(8,128)(2,1)}, u32[]{:S(2)}, u32[]{:S(2)}) collective-permute-start(bf16[64,1000]{1,0:T(8,128)(2,1)} %bitcast_convert_fusion), channel_id=1, source_target_pairs={{0,16},{16,32},{32,48},{48,64},{64,80},{80,96},{96,112},{112,128},... | collective-permute-start | bytes 384008 | tf_op jit(solution)/shard_map/ppermute | solution.py:41
  185.4 1.3 collective-permute-start.5
  188.0 67.1 %reduce-scatter.4.cloned.1.call-done = bf16[64,3048]{1,0:T(8,128)(2,1)} async-done(((bf16[1024,3048]{1,0:T(8,128)(2,1)}), bf16[64,3048]{1,0:T(8,128)(2,1)}) %reduce-scatter.4.cloned.1.call-update) | async-done | bytes 390160 | tf_op jit(solution)/shard_map/reduce_scatter | solution.py:31
  255.1 2.4 multiply_reduce_fusion.11
  258.8 1.9 multiply_reduce_fusion.10
  270.8 9.8 %all-reduce.1 = (f32[]{:T(128)}, f32[]{:T(128)}, f32[]{:T(128)}, f32[]{:T(128)}, f32[]{:T(128)}, /*index=5*/f32[]{:T(128)}, f32[]{:T(128)}) all-reduce(f32[]{:T(128)S(6)} %add.155, f32[]{:T(128)S(6)} %add.152, f32[]{:T(128)S(6)} %add.172, f32[]{:T(128)S(6)} %add.166, ...), channel_id=1, replica_groups=mesh['chain'=16,'dp_0'=4,'dp_1'=4] {'dp_0'}, use_global_device_ids=true, to_apply=%region_8.9 | all-reduce | flops 7 | bytes 56 | tf_op jit(solution)/shard_map/psum | solution.py:46
  280.6 10.1 %all-reduce = (f32[]{:T(128)}, f32[]{:T(128)}, f32[]{:T(128)}, f32[]{:T(128)}, f32[]{:T(128)}, /*index=5*/f32[]{:T(128)}, f32[1]{0:T(128)}) all-reduce(f32[]{:T(128)} %get-tuple-element.43, f32[]{:T(128)} %get-tuple-element.44, f32[]{:T(128)} %get-tuple-element.45, ...), channel_id=1, replica_groups=mesh['chain'=16,'dp_0'=4,'dp_1'=4] {'dp_1'}, use_global_device_ids=true, to_apply=%region_9.10 | all-reduce | flops 7 | bytes 56 | tf_op jit(solution)/shard_map/psum | solution.py:46
  294.8 7.1 %all-to-all-start = ((f32[16,1,2]{2,1,0:T(1,128)}), f32[16,1,2]{2,1,0:T(1,128)S(1)}, u32[]{:S(2)}, u32[]{:S(2)}) async-start(f32[16,1,2]{2,1,0:T(1,128)} %broadcast_in_dim.29), calls=%async_computation | async-start | bytes 16384 | tf_op jit(solution)/shard_map/all_to_all | solution.py:58
  303.3 6.2 %all-to-all-done = f32[16,1,2]{2,1,0:T(1,128)S(1)} async-done(((f32[16,1,2]{2,1,0:T(1,128)}), f32[16,1,2]{2,1,0:T(1,128)S(1)}, u32[]{:S(2)}, u32[]{:S(2)}) %all-to-all-start) | async-done | bytes 160 | tf_op jit(solution)/shard_map/all_to_all | solution.py:58
  315.4 1.0 fusion.8
  (58 shorter events, 7.6 us)
Async XLA Ops:
  7.2 44.9 %copy-start.9 = (s32[1,896]{1,0:T(1,128)S(1)}, s32[1,896]{1,0:T(1,128)}, u32[]{:S(2)}) copy-start(s32[1,896]{1,0:T(1,128)} %param.17) | copy-start | bytes 10756
  7.2 52.8 %all-gather.4.cloned.1.call-start = ((), (), s32[]{:S(2)}) async-start(), calls=%async_computation.2 | async-start | bytes 2621440 | tf_op jit(solution)/shard_map/all_gather | solution.py:25
  22.5 71.3 %all-gather.6.cloned.1.call-start = ((), (), s32[]{:S(2)}) async-start(), calls=%async_computation.3 | async-start | bytes 2621440 | tf_op jit(solution)/shard_map/all_gather | solution.py:25
  37.5 91.6 %all-gather.8.cloned.1.call-start = ((), (), s32[]{:S(2)}) async-start(), calls=%async_computation.4 | async-start | bytes 2621440 | tf_op jit(solution)/shard_map/all_gather | solution.py:25
  52.1 203.1 %reduce-scatter.4.cloned.1.call-start = ((), (), s32[]{:S(2)}) async-start(), calls=%async_computation.5 | async-start | bytes 6684672 | tf_op jit(solution)/shard_map/reduce_scatter | solution.py:31
  52.2 7.7 %copy-start.10 = (s32[1,896]{1,0:T(1,128)S(1)}, s32[1,896]{1,0:T(1,128)}, u32[]{:S(2)}) copy-start(s32[1,896]{1,0:T(1,128)} %param.18) | copy-start | bytes 10756
  59.9 33.9 %copy-start.3 = (bf16[896,1024]{1,0:T(8,128)(2,1)}, bf16[896,1024]{1,0:T(8,128)(2,1)S(1)}, u32[]{:S(2)}) copy-start(bf16[896,1024]{1,0:T(8,128)(2,1)S(1)} %gather_fusion) | copy-start | bytes 5505028
  100.0 34.7 %copy-start.13 = (bf16[896,1024]{1,0:T(8,128)(2,1)S(1)}, bf16[896,1024]{1,0:T(8,128)(2,1)}, u32[]{:S(2)}) copy-start(bf16[896,1024]{1,0:T(8,128)(2,1)} %add_convert_fusion) | copy-start | bytes 5505028
  134.7 3.6 %copy-start.11 = (bf16[1024,1000]{1,0:T(8,128)(2,1)S(1)}, bf16[1024,1000]{1,0:T(8,128)(2,1)}, u32[]{:S(2)}) copy-start(bf16[1024,1000]{1,0:T(8,128)(2,1)} %all-gather.8.cloned.1.call-done) | copy-start | bytes 6144004
  138.3 3.4 %copy-start.12 = (f32[896,1024]{1,0:T(8,128)S(1)}, f32[896,1024]{1,0:T(8,128)}, u32[]{:S(2)}) copy-start(f32[896,1024]{1,0:T(8,128)} %fusion.23) | copy-start | bytes 11010052
  140.4 1.2 copy-start.14
  168.6 0.9 copy-start.2
  168.6 4.0 %copy-start.1 = (f32[1,64,1024]{2,1,0:T(8,128)S(1)}, f32[1,64,1024]{2,1,0:T(8,128)}, u32[]{:S(2)}) copy-start(f32[1,64,1024]{2,1,0:T(8,128)} %param.11) | copy-start | bytes 786436
  168.6 9.9 %copy-start = (f32[1,64,1000]{2,1,0:T(8,128)S(1)}, f32[1,64,1000]{2,1,0:T(8,128)}, u32[]{:S(2)}) copy-start(f32[1,64,1000]{2,1,0:T(8,128)} %param.12) | copy-start | bytes 768004
  168.6 86.5 %copy-start.6 = (f32[2,64,1024]{2,1,0:T(8,128)S(1)}, f32[2,64,1024]{2,1,0:T(8,128)}, u32[]{:S(2)}) copy-start(f32[2,64,1024]{2,1,0:T(8,128)} %param.14) | copy-start | bytes 1572868
  169.6 89.2 %copy-start.5 = (f32[2,64,1000]{2,1,0:T(8,128)S(1)}, f32[2,64,1000]{2,1,0:T(8,128)}, u32[]{:S(2)}) copy-start(f32[2,64,1000]{2,1,0:T(8,128)} %param.15) | copy-start | bytes 1536004
  169.6 15.8 %collective-permute-start = (bf16[64,1024]{1,0:T(8,128)(2,1)S(1)}, bf16[64,1024]{1,0:T(8,128)(2,1)S(1)}, u32[]{:S(2)}, u32[]{:S(2)}) collective-permute-start(bf16[64,1024]{1,0:T(8,128)(2,1)S(1)} %bitcast_convert_fusion.2), channel_id=1, source_target_pairs={{0,16},{16,32},{32,48},{48,64},{64,80},{80,96},{96,112},{112,128},... | collective-permute-start | bytes 393224 | tf_op jit(solution)/shard_map/ppermute | solution.py:41
  171.3 15.4 %collective-permute-start.3 = (bf16[64,1024]{1,0:T(8,128)(2,1)S(1)}, bf16[64,1024]{1,0:T(8,128)(2,1)S(1)}, u32[]{:S(2)}, u32[]{:S(2)}) collective-permute-start(bf16[64,1024]{1,0:T(8,128)(2,1)S(1)} %bitcast_convert_fusion.2), channel_id=1, source_target_pairs={{16,0},{32,16},{48,32},{64,48},{80,64},{96,80},{112,96},{128,112},... | collective-permute-start | bytes 393224 | tf_op jit(solution)/shard_map/ppermute | solution.py:41
  172.6 14.0 %collective-permute-start.1 = (bf16[64,1024]{1,0:T(8,128)(2,1)S(1)}, bf16[64,1024]{1,0:T(8,128)(2,1)S(1)}, u32[]{:S(2)}, u32[]{:S(2)}) collective-permute-start(bf16[64,1024]{1,0:T(8,128)(2,1)S(1)} %bitcast_convert_fusion.1), channel_id=1, source_target_pairs={{0,16},{16,32},{32,48},{48,64},{64,80},{80,96},{96,112},{112,128},... | collective-permute-start | bytes 393224 | tf_op jit(solution)/shard_map/ppermute | solution.py:41
  177.2 9.5 %collective-permute-start.4 = (bf16[64,1024]{1,0:T(8,128)(2,1)S(1)}, bf16[64,1024]{1,0:T(8,128)(2,1)S(1)}, u32[]{:S(2)}, u32[]{:S(2)}) collective-permute-start(bf16[64,1024]{1,0:T(8,128)(2,1)S(1)} %bitcast_convert_fusion.1), channel_id=1, source_target_pairs={{16,0},{32,16},{48,32},{64,48},{80,64},{96,80},{112,96},{128,112},... | collective-permute-start | bytes 393224 | tf_op jit(solution)/shard_map/ppermute | solution.py:41
  179.2 79.6 %collective-permute-start.2 = (bf16[64,1000]{1,0:T(8,128)(2,1)}, bf16[64,1000]{1,0:T(8,128)(2,1)}, u32[]{:S(2)}, u32[]{:S(2)}) collective-permute-start(bf16[64,1000]{1,0:T(8,128)(2,1)} %bitcast_convert_fusion), channel_id=1, source_target_pairs={{0,16},{16,32},{32,48},{48,64},{64,80},{80,96},{96,112},{112,128},... | collective-permute-start | bytes 384008 | tf_op jit(solution)/shard_map/ppermute | solution.py:41
  185.4 73.4 %collective-permute-start.5 = (bf16[64,1000]{1,0:T(8,128)(2,1)}, bf16[64,1000]{1,0:T(8,128)(2,1)}, u32[]{:S(2)}, u32[]{:S(2)}) collective-permute-start(bf16[64,1000]{1,0:T(8,128)(2,1)} %bitcast_convert_fusion), channel_id=1, source_target_pairs={{16,0},{32,16},{48,32},{64,48},{80,64},{96,80},{112,96},{128,112},... | collective-permute-start | bytes 384008 | tf_op jit(solution)/shard_map/ppermute | solution.py:41
  186.7 0.7 copy-start.7
  187.3 0.7 copy-start.8
  255.1 59.5 %copy-start.4 = (bf16[64,3048]{1,0:T(8,128)(2,1)S(1)}, bf16[64,3048]{1,0:T(8,128)(2,1)}, u32[]{:S(2)}) copy-start(bf16[64,3048]{1,0:T(8,128)(2,1)} %reduce-scatter.4.cloned.1.call-done) | copy-start | bytes 1170436
  294.8 14.7 %all-to-all-start = ((f32[16,1,2]{2,1,0:T(1,128)}), f32[16,1,2]{2,1,0:T(1,128)S(1)}, u32[]{:S(2)}, u32[]{:S(2)}) async-start(f32[16,1,2]{2,1,0:T(1,128)} %broadcast_in_dim.29), calls=%async_computation | async-start | bytes 16384 | tf_op jit(solution)/shard_map/all_to_all | solution.py:58
Sparse Core Ops, SparseCore 0:
  22.6 35.9 all-gather.3
  60.4 33.3 all-gather.5
  95.6 33.3 all-gather.7
  168.8 86.3 reduce-scatter.3
where the time goes:
time: 327 us; the launch traced here: 325 us
  waiting for transfers between devices  130 us (40%)
  blocking collectives  61.6 us (19%)
  between operations  37 us (11%)
  matrix products  36.2 us (11%)
  starting transfers between devices  22.3 us (7%)
  local copies, waits for them, and re-layouts  21.2 us (6%)
  other arithmetic  16.6 us (5%)
    reduce_scatter x1, waiting for transfers between devices, in_one_piece(): lax.psum_scatter(both, axis, scatter_dimension=dim, tiled=True)  67.1 us
    all_gather x3, waiting for transfers between devices, gather_axes(): nearer = lax.all_gather(value, axes[-1], axis=dim, tiled=True)  56.9 us
    all_gather x3, blocking collectives, gather_axes(): nearer = lax.all_gather(value, axes[-1], axis=dim, tiled=True)  41.7 us
    psum x2, blocking collectives, over_axes(): value = lax.psum(value, axis)  19.9 us
    dot_general x3, matrix products, dot_tn(): lax.dot_general(left, right, (((0,), (0,)), ((), ())), preferred_element_...  16.2 us
    ppermute x6, starting transfers between devices, passed_along(): return lax.ppermute(block, axis, route)  15 us
    unnamed x31, local copies, waits for them, and re-layouts  12.3 us
    gather x1, local copies, waits for them, and re-layouts, on_device(): rows = data_pool[batch_rows[0]]  7.73 us
  transfers between devices with their start and end apart: 11, of which 4 were waited for; matrix products, arithmetic and copies ran while one was open for 8% of the time, Pallas kernels for 0%

commit v1 on v0

v1 whole, which is shorter than its diff:
```python
import functools

import jax
import jax.numpy as jnp
from jax import lax
from jax.experimental import pallas as pl
from jax.experimental.pallas import tpu as pltpu
from jax.sharding import Mesh
from jax.sharding import PartitionSpec as P

DP = ("dp_0", "dp_1")
SPRING = 0.03
EPS = 1e-06
F32 = jnp.float32
BF16 = jnp.bfloat16
SIDE = 4
N_COPIES = 260


def mm(a, b):
    return jnp.dot(a, b, preferred_element_type=F32)


def mm_nt(a, b):
    return lax.dot_general(a, b, (((1,), (1,)), ((), ())), preferred_element_type=F32)


def mm_tn(a, b):
    return lax.dot_general(a, b, (((0,), (0,)), ((), ())), preferred_element_type=F32)


class Copies:
    def __init__(self, send, recv):
        self.send, self.recv, self.all = send, recv, []

    def start(self, src, dst, device):
        i = len(self.all)
        copy = pltpu.make_async_remote_copy(
            src_ref=src,
            dst_ref=dst,
            send_sem=self.send.at[i],
            recv_sem=self.recv.at[i],
            device_id=device,
            device_id_type=pl.DeviceIdType.MESH,
        )
        copy.start()
        self.all.append(copy)
        return copy


def kernel(
    dims,
    im_in, im_mid, im_out, en_in, en_mid, en_out, pool_hbm, rows_ref, labs_ref, climb_ref,
    up_in, up_mid, up_out, tab_ref,
    W, G, RA1, RAd, RAs, R1, RB1, RBd, RBs, gsh,
    own_in, own_mid, own_out, nb_in, nb_mid, nb_out, e_in, e_mid, e_out, AH, BH,
    pool, onehot, rcol, lcol, x, hid, slope, resid, dlog, dres, dpre,
    mine, sums, chain_mine, chain_tab,
    local_sem, send_sem, recv_sem,
):
    chain_n, batch, classes = dims
    rows = x.shape[0]
    width = x.shape[1]
    half_rows = rows // 2
    ci = lax.axis_index("chain")
    yi = lax.axis_index("dp_0")
    xi = lax.axis_index("dp_1")
    cp = Copies(send_sem, recv_sem)

    def at_x(step):
        return {"dp_1": lax.rem(xi + step, SIDE)}

    def at_y(step):
        return {"dp_0": lax.rem(yi + step, SIDE)}

    def xs(step):
        return lax.rem(xi + step, SIDE)

    def ys(step):
        return lax.rem(yi + step, SIDE)

    def at_chain(step):
        return {"chain": lax.rem(ci + step, chain_n)}

    loads = []

    def load(src, dst):
        c = pltpu.make_async_copy(src, dst, local_sem.at[len(loads)])
        c.start()
        loads.append(c)

    load(im_in.at[0], own_in)
    load(im_mid.at[0], own_mid)
    load(im_out.at[0], own_out)
    load(pool_hbm, pool)
    load(en_in, e_in)
    load(en_mid, e_mid)
    load(en_out, e_out)

    barrier = pltpu.get_barrier_semaphore()
    partners = [at_x(s) for s in (1, 2, 3)] + [at_y(s) for s in (1, 2, 3)]
    partners += [at_chain(s) for s in range(1, chain_n)]
    for device in partners:
        pl.semaphore_signal(barrier, inc=1, device_id=device, device_id_type=pl.DeviceIdType.MESH)

    factors = (width ** (-0.5), hid.shape[1] ** (-0.5), width ** (-0.5))
    edge = classes // 128 * 128
    for m, ref in enumerate((own_in, own_mid, own_out)):
        loads[m].wait()
        if m == 2:
            W[m, yi, xi, :, :, edge:] = jnp.zeros((2, 32, width - edge), BF16)
        n = ref.shape[1]
        W[m, yi, xi, :, :, :n] = (ref[...] * factors[m]).astype(BF16).reshape(2, 32, n)
    pl.semaphore_wait(barrier, len(partners))

    DIRS = (1, 3)

    def near(h, d):
        return at_x(d) if h == 0 else at_y(d)

    def far(h, d):
        return at_y(d) if h == 0 else at_x(d)

    def w_near(m, h, step):
        return W.at[m, yi, xs(step), h] if h == 0 else W.at[m, ys(step), xi, h]

    def w_near_half(m, h, step, k):
        r = pl.ds(16 * k, 16)
        return W.at[m, yi, xs(step), h, r] if h == 0 else W.at[m, ys(step), xi, h, r]

    def blocks(ref, m, h, step, k, cols=None):
        two = pl.ds(2 * k, 2)
        cols = pl.ds(0, ref.shape[-1]) if cols is None else cols
        if h == 0:
            return ref.at[m, ys(step), two, 0, :, cols]
        return ref.at[m, two, xs(step), 1, :, cols]

    BOTH = [(h, k) for h in (0, 1) for k in (0, 1)]
    p1, p1f, p2a, p2b, p2f = {}, {}, {}, {}, {}
    for m in range(3):
        for h, k in BOTH:
            src = w_near(m, h, 0)
            p1[m, h, k] = cp.start(src, src, near(h, DIRS[k]))

    nb = []
    for own, buf in ((own_in, nb_in), (own_mid, nb_mid), (own_out, nb_out)):
        nb.append(cp.start(own, buf.at[0], at_chain(1)))
        nb.append(cp.start(own, buf.at[1], at_chain(chain_n - 1)))

    def ag_near_forward(m):
        for h, k in BOTH:
            p1[m, h, k].wait_recv()
            src = w_near_half(m, h, SIDE - DIRS[k], k)
            p1f[m, h, k] = cp.start(src, src, near(h, DIRS[k]))

    def ag_far_start(m):
        for h, k in BOTH:
            p1f[m, h, k].wait_recv()
        for h, k in BOTH:
            src = blocks(W, m, h, 0, k)
            p2a[m, h, k] = cp.start(src, src, far(h, DIRS[k]))
        for h, k in BOTH:
            src = blocks(W, m, h, 0, 1 - k)
            p2b[m, h, k] = cp.start(src, src, far(h, DIRS[k]))

    def ag_far_forward(m):
        for h, k in BOTH:
            p2a[m, h, k].wait_recv()
            src = blocks(W, m, h, SIDE - DIRS[k], k)
            p2f[m, h, k] = cp.start(src, src, far(h, DIRS[k]))

    def ag_end(m):
        for h, k in BOTH:
            p2b[m, h, k].wait_recv()
            p2f[m, h, k].wait_recv()

    def weight(m):
        return W[m].reshape(width, width)

    def part(i):
        return pl.ds(i * half_rows, half_rows)

    for ref, col in ((rows_ref, rcol), (labs_ref, lcol)):
        for k in range(rows // 128):
            r = pl.ds(k * 128, 128)
            col[r, :] = jnp.transpose(jnp.broadcast_to(ref[:, r].astype(F32), (128, 128)))

    def lanes(c):
        return (lax.broadcasted_iota(jnp.int32, (1, 128), 1) + 128 * c).astype(F32)

    def pick_rows(i):
        for c in range(pool.shape[0] // 128):
            hit = rcol[part(i), :] == lanes(c)
            onehot[part(i), c * 128 : (c + 1) * 128] = jnp.where(hit, 1.0, 0.0).astype(BF16)
        x[part(i), :] = mm(onehot[part(i), :], pool[...]).astype(BF16)

    loads[3].wait()
    pick_rows(0)
    ag_near_forward(0)
    pick_rows(1)
    ag_near_forward(1)
    ag_near_forward(2)
    ag_far_start(0)

    for c in loads[4:]:
        c.wait()
    for c in nb:
        c.wait_recv()
    first, last = ci == 0, ci == chain_n - 1
    own = (own_in, own_mid, own_out)
    sq_a = sq_b = cross = jnp.zeros((1, 128), F32)

    def fold(v):
        v = jnp.sum(v, axis=0, keepdims=True)
        out = v[:, :128]
        for c in range(1, v.shape[1] // 128):
            out = out + v[:, c * 128 : (c + 1) * 128]
        return out

    for m, (e, b) in enumerate(((e_in, nb_in), (e_mid, nb_mid), (e_out, nb_out))):
        n = own[m].shape[1]
        o = own[m][...]
        if m == 2:
            AH[m, :, edge:] = jnp.zeros((o.shape[0], width - edge), F32)
            BH[m, :, edge:] = jnp.zeros((o.shape[0], width - edge), F32)
        AH[m, :, :n] = jnp.where(last, e[1], b[1]) - o
        BH[m, :, :n] = o - jnp.where(first, e[0], b[0])
        a, z = AH[m], BH[m]
        sq_a, sq_b, cross = sq_a + fold(a * a), sq_b + fold(z * z), cross + fold(a * z)

    def pack(*values):
        zero = jnp.zeros((8 - len(values), 128), F32)
        return jnp.concatenate([*values, zero], axis=0)

    def exchange(slot, tile, index, peers):
        mine[slot] = tile
        return [cp.start(mine.at[slot], sums.at[slot, index], device) for device in peers]

    def collect(slot, copies, index):
        for c in copies:
            c.wait_recv()
        sums[slot, index] = mine[slot]
        out = sums[slot, 0]
        for k in range(1, SIDE):
            out = out + sums[slot, k]
        return out

    x_peers = [at_x(s) for s in (1, 2, 3)]
    y_peers = [at_y(s) for s in (1, 2, 3)]
    early_x = exchange(0, pack(sq_b, sq_a, cross), xi, x_peers)
    ag_far_forward(0)
    ag_far_start(1)
    early_y = exchange(1, collect(0, early_x, xi), yi, y_peers)
    early = jnp.sum(collect(1, early_y, yi), axis=1, keepdims=True)
    sq_behind = jnp.broadcast_to(early[0:1], (1, 128))
    sq_ahead = jnp.broadcast_to(early[1:2], (1, 128))
    cross = jnp.broadcast_to(early[2:3], (1, 128))
    len_ahead = jnp.sqrt(sq_ahead + EPS)
    len_behind = jnp.sqrt(sq_behind + EPS)
    raw_sq = (
        sq_ahead / (len_ahead * len_ahead)
        + sq_behind / (len_behind * len_behind)
        + 2.0 * cross / (len_ahead * len_behind)
    )
    raw_len = jnp.sqrt(raw_sq + EPS)
    tau_sq = raw_sq / (raw_sq + EPS)
    chain_mine[...] = pack(len_behind, len_ahead)
    lengths = [
        cp.start(chain_mine, chain_tab.at[ci], at_chain(s)) for s in range(1, chain_n)
    ]

    def forward_in(i):
        pre = mm(x[part(i), :], weight(0))
        sig = jax.nn.sigmoid(pre)
        hid[part(i), :] = (pre * sig).astype(BF16)
        slope[part(i), :] = sig * (1.0 + pre * (1.0 - sig))

    def forward_mid(i):
        r = x[part(i), :].astype(F32) + mm(hid[part(i), :], weight(1))
        resid[part(i), :] = r.astype(BF16)

    norm = 1.0 / (batch * classes)

    def forward_out(i, energy):
        logits = mm(resid[part(i), :], weight(2))
        for c in range(width // 128):
            hit = lcol[part(i), :] == lanes(c)
            err = logits[:, c * 128 : (c + 1) * 128] - jnp.where(hit, 1.0, 0.0)
            energy = energy + jnp.sum(err * err, axis=0, keepdims=True)
            dlog[part(i), c * 128 : (c + 1) * 128] = (err * norm).astype(BF16)
        return energy

    ag_end(0)
    forward_in(0)
    ag_far_forward(1)
    ag_far_start(2)
    forward_in(1)
    for c in lengths:
        c.wait_recv()
    chain_tab[ci] = chain_mine[...]
    arc = jnp.zeros((1, 128), F32)
    band = jnp.zeros((1, 128), F32)
    for j in range(chain_n):
        piece = chain_tab[j, 0:1]
        arc = arc + jnp.where(j <= ci, piece, 0.0)
        band = band + piece
    band = band + chain_tab[chain_n - 1, 1:2]
    ag_end(1)
    forward_mid(0)
    forward_mid(1)
    ag_far_forward(2)
    ag_end(2)
    energy = forward_out(0, jnp.zeros((1, 128), F32))
    energy = forward_out(1, energy)

    COLS = width // 2
    PIECES = [(m, c) for m in (2, 1, 0) for c in (0, 1)]

    def cols_of(c):
        return pl.ds(c * COLS, COLS)

    def grad(p, left, right):
        m, c = PIECES[p]
        g = mm_tn(left[...], right[:, cols_of(c)]).astype(BF16)
        G[m, :, :, :, :, cols_of(c)] = g.reshape(SIDE, SIDE, 2, 32, COLS)

    a1, ad, a_s, b1, bd, bs = {}, {}, {}, {}, {}, {}

    def rs_start(p):
        m, c = PIECES[p]
        q = cols_of(c)
        for h, k in BOTH:
            dst = RA1.at[m, h, k, :, :, q]
            a1[p, h, k] = cp.start(blocks(G, m, h, 2, k, q), dst, far(h, DIRS[k]))
        for h, k in BOTH:
            dst = RAd.at[m, h, k, :, :, q]
            src = blocks(G, m, h, DIRS[k], 1 - k, q)
            ad[p, h, k] = cp.start(src, dst, far(h, DIRS[k]))

    def rs_far_sum(p):
        m, c = PIECES[p]
        q = cols_of(c)
        for h, k in BOTH:
            a1[p, h, k].wait_recv()
            mid = RA1.at[m, h, k, :, :, q]
            own_g = blocks(G, m, h, DIRS[k], k, q)
            mid[...] = (mid[...].astype(F32) + own_g[...].astype(F32)).astype(BF16)
            a_s[p, h, k] = cp.start(mid, RAs.at[m, h, k, :, :, q], far(h, DIRS[k]))

    def rs_near_start(p):
        m, c = PIECES[p]
        q = cols_of(c)
        for h in (0, 1):
            for k in (0, 1):
                ad[p, h, k].wait_recv()
                a_s[p, h, k].wait_recv()
            for k in (0, 1):
                total = blocks(G, m, h, 0, k, q)[...].astype(F32)
                total = total + RAs[m, h, k, :, :, q].astype(F32)
                total = total + RAd[m, h, 1 - k, :, :, q].astype(F32)
                R1[m, h, pl.ds(2 * k, 2), :, q] = total.astype(BF16)
            for k in (0, 1):
                step = ys if h else xs
                src = R1.at[m, h, step(2), pl.ds(16 * k, 16), q]
                b1[p, h, k] = cp.start(src, RB1.at[m, h, k, :, q], near(h, DIRS[k]))
            for k in (0, 1):
                src = R1.at[m, h, step(DIRS[k]), pl.ds(16 * (1 - k), 16), q]
                bd[p, h, k] = cp.start(src, RBd.at[m, h, k, :, q], near(h, DIRS[k]))

    def rs_near_sum(p):
        m, c = PIECES[p]
        q = cols_of(c)
        for h, k in BOTH:
            step = ys if h else xs
            b1[p, h, k].wait_recv()
            mid = RB1.at[m, h, k, :, q]
            own_r = R1[m, h, step(DIRS[k]), pl.ds(16 * k, 16), q]
            mid[...] = (mid[...].astype(F32) + own_r.astype(F32)).astype(BF16)
            bs[p, h, k] = cp.start(mid, RBs.at[m, h, k, :, q], near(h, DIRS[k]))

    dots = [jnp.zeros((1, 128), F32)] * 3

    def rs_end(p):
        m, c = PIECES[p]
        q = cols_of(c)
        for h in (0, 1):
            step = ys if h else xs
            for k in (0, 1):
                bd[p, h, k].wait_recv()
                bs[p, h, k].wait_recv()
            for k in (0, 1):
                total = R1[m, h, step(0), pl.ds(16 * k, 16), q].astype(F32)
                total = total + RBs[m, h, k, :, q].astype(F32)
                total = total + RBd[m, h, 1 - k, :, q].astype(F32)
                g = total * factors[m]
                r = pl.ds(32 * h + 16 * k, 16)
                gsh[m, r, q] = g
                dots[0] = dots[0] + fold(g * AH[m, r, q])
                dots[1] = dots[1] + fold(g * BH[m, r, q])
                dots[2] = dots[2] + fold(g * g)

    def back_resid(i):
        dres[part(i), :] = mm_nt(dlog[part(i), :], weight(2)).astype(BF16)

    def back_pre(i):
        d = mm_nt(dres[part(i), :], weight(1)) * slope[part(i), :]
        dpre[part(i), :] = d.astype(BF16)

    grad(0, resid, dlog)
    rs_start(0)
    grad(1, resid, dlog)
    rs_start(1)
    back_resid(0)
    rs_far_sum(0)
    back_resid(1)
    rs_far_sum(1)
    grad(2, hid, dres)
    rs_start(2)
    grad(3, hid, dres)
    rs_start(3)
    back_pre(0)
    rs_far_sum(2)
    back_pre(1)
    grad(4, x, dpre)
    rs_start(4)
    rs_far_sum(3)
    grad(5, x, dpre)
    rs_start(5)
    rs_near_start(0)
    rs_far_sum(4)
    rs_near_start(1)
    rs_far_sum(5)
    rs_near_start(2)
    rs_near_sum(0)
    rs_near_start(3)
    rs_near_sum(1)
    rs_near_start(4)
    rs_near_sum(2)
    rs_near_start(5)
    rs_near_sum(3)
    rs_end(0)
    rs_end(1)
    rs_near_sum(4)
    rs_end(2)
    rs_near_sum(5)
    rs_end(3)
    rs_end(4)
    rs_end(5)

    late_x = exchange(2, pack(*dots, energy), xi, x_peers)
    late_y = exchange(3, collect(2, late_x, xi), yi, y_peers)
    late = jnp.sum(collect(3, late_y, yi), axis=1, keepdims=True)
    g_ahead, g_behind, g_g, energy = (
        jnp.broadcast_to(late[k : k + 1], (1, 128)) for k in range(4)
    )
    along = (g_ahead / len_ahead + g_behind / len_behind) / raw_len
    count = float(chain_n)
    goal = (ci + 1).astype(F32) / (count + 1.0) * band
    climbing = climb_ref[:, 0:1] == 1
    coef = jnp.where(climbing, 2.0 * along, along + SPRING * (goal - arc) / band)
    force_sq = g_g - 2.0 * coef * along + coef * coef * tau_sq
    scale = band / (count + 1.0) / jnp.sqrt(force_sq + EPS)
    wa = (scale * coef / (len_ahead * raw_len))[:, 0:1]
    wb = (scale * coef / (len_behind * raw_len))[:, 0:1]
    scale = scale[:, 0:1]
    for m, up in enumerate((up_in, up_mid, up_out)):
        n = up.shape[1]
        u = wa * AH[m, :, :n] + wb * BH[m, :, :n] - scale * gsh[m, :, :n]
        up[...] = own[m][...] + u
    tab_ref[...] = pack(0.5 * norm * energy, arc / band, 0.5 * raw_len)
    for c in cp.all:
        c.wait_send()


def on_device(
    images_in, images_mid, images_out, ends_in, ends_mid, ends_out, data_pool, batch_rows, labels, climbing
):
    _, shard, hidden_units = images_in.shape
    width = data_pool.shape[1]
    classes = images_out.shape[2]
    rows = batch_rows.shape[1]
    pool_rows = data_pool.shape[0]
    chain_n = lax.axis_size("chain")
    batch = rows * lax.axis_size(DP)
    any_spec = pl.BlockSpec(memory_space=pl.ANY)
    vmem_spec = pl.BlockSpec(memory_space=pltpu.VMEM)
    vm = pltpu.VMEM
    scratch = [
        vm((3, SIDE, SIDE, 2, 32, width), BF16),
        vm((3, SIDE, SIDE, 2, 32, width), BF16),
        vm((3, 2, 2, 2, 32, width), BF16),
        vm((3, 2, 2, 2, 32, width), BF16),
        vm((3, 2, 2, 2, 32, width), BF16),
        vm((3, 2, SIDE, 32, width), BF16),
        vm((3, 2, 2, 16, width), BF16),
        vm((3, 2, 2, 16, width), BF16),
        vm((3, 2, 2, 16, width), BF16),
        vm((3, shard, width), F32),
        vm((shard, width), F32),
        vm((shard, width), F32),
        vm((shard, classes), F32),
        vm((2, shard, width), F32),
        vm((2, shard, width), F32),
        vm((2, shard, classes), F32),
        vm((2, shard, width), F32),
        vm((2, shard, width), F32),
        vm((2, shard, classes), F32),
        vm((3, shard, width), F32),
        vm((3, shard, width), F32),
        vm((pool_rows, width), BF16),
        vm((rows, pool_rows), BF16),
        vm((rows, 128), F32),
        vm((rows, 128), F32),
        vm((rows, width), BF16),
        vm((rows, width), BF16),
        vm((rows, width), F32),
        vm((rows, width), BF16),
        vm((rows, width), BF16),
        vm((rows, width), BF16),
        vm((rows, width), BF16),
        vm((4, 8, 128), F32),
        vm((4, SIDE, 8, 128), F32),
        vm((8, 128), F32),
        vm((chain_n, 8, 128), F32),
        pltpu.SemaphoreType.DMA((7,)),
        pltpu.SemaphoreType.DMA((N_COPIES,)),
        pltpu.SemaphoreType.DMA((N_COPIES,)),
    ]
    climb = jnp.broadcast_to(climbing[:, None], (1, 128))
    up_in, up_mid, up_out, tab = pl.pallas_call(
        functools.partial(kernel, (chain_n, batch, classes)),
        out_shape=(
            jax.ShapeDtypeStruct((shard, hidden_units), F32),
            jax.ShapeDtypeStruct((shard, width), F32),
            jax.ShapeDtypeStruct((shard, classes), F32),
            jax.ShapeDtypeStruct((8, 128), F32),
        ),
        in_specs=[any_spec] * 7 + [vmem_spec] * 3,
        out_specs=(vmem_spec,) * 4,
        scratch_shapes=scratch,
        compiler_params=pltpu.CompilerParams(
            collective_id=0, has_side_effects=True, vmem_limit_bytes=60 * 2**20
        ),
        cost_estimate=pl.CostEstimate(
            flops=2 * rows * width * (8 * width + pool_rows), bytes_accessed=10**7, transcendentals=10**6
        ),
        name="band_step",
    )(images_in, images_mid, images_out, ends_in, ends_mid, ends_out, data_pool, batch_rows, labels, climb)
    return (up_in[None], up_mid[None], up_out[None], tab[0, 0:1], tab[1, 0:1], tab[2, 0:1])


def solution(mesh):
    torus = Mesh(mesh.devices.reshape(mesh.shape["chain"], SIDE, SIDE), ("chain", "dp_0", "dp_1"))
    shard = P("chain", DP, None)
    end = P(None, DP, None)
    in_specs = (
        shard, shard, shard, end, end, end, P(DP, None), P("chain", DP), P("chain", DP), P("chain"),
    )
    out_specs = (shard, shard, shard, P("chain"), P("chain"), P("chain"))
    return jax.shard_map(
        on_device, mesh=torus, in_specs=in_specs, out_specs=out_specs, check_vma=False
    )
```

time: 327 us -> 111 us (0.34)
  waiting for transfers between devices: 130 us -> 0 us
  Pallas kernels: 0 us -> 102 us
  blocking collectives: 61.6 us -> 0 us
  matrix products: 36.2 us -> 0 us
  between operations: 37 us -> 1.29 us
  starting transfers between devices: 22.3 us -> 0 us
  other arithmetic: 16.6 us -> 0 us
  local copies, waits for them, and re-layouts: 21.2 us -> 6.83 us
    pallas_call x0 -> x1, Pallas kernels: none -> 102 us  [on_device(): pl.pallas_call(functools.partial(kernel, (chain_n, batch, classes)), out_...]
    reduce_scatter x1 -> x0, waiting for transfers between devices: 67.1 us -> none  [in_one_piece(): lax.psum_scatter(both, axis, scatter_dimension=dim, tiled=True)]
    all_gather x3 -> x0, waiting for transfers between devices: 56.9 us -> none  [gather_axes(): nearer = lax.all_gather(value, axes[-1], axis=dim, tiled=True)]
    all_gather x3 -> x0, blocking collectives: 41.7 us -> none  [gather_axes(): nearer = lax.all_gather(value, axes[-1], axis=dim, tiled=True)]
    dot_general x7 -> x0, matrix products: 36.2 us -> none  [the longest x3 16.2 us: dot_tn(): lax.dot_general(left, right, (((0,), (0,)), ((), ())), preferred_element_...]
    psum x2 -> x0, blocking collectives: 19.9 us -> none  [over_axes(): value = lax.psum(value, axis)]
    ppermute x6 -> x0, starting transfers between devices: 15 us -> none  [passed_along(): return lax.ppermute(block, axis, route)]
    gather x1 -> x0, local copies, waits for them, and re-layouts: 7.73 us -> none  [on_device(): rows = data_pool[batch_rows[0]]]
  transfers between devices with their start and end apart: 11 -> 0, of which waited for: 4 -> 0; matrix products, arithmetic and copies ran while one was open for 8% -> 0% of each run, Pallas kernels for 0% -> 0%
where the time goes in v1:
time: 111 us
  Pallas kernels  102 us (92%)
  local copies, waits for them, and re-layouts  6.83 us (6%)
  between operations  1.29 us (1%)
    pallas_call x1, Pallas kernels, on_device(): pl.pallas_call(functools.partial(kernel, (chain_n, batch, classes)), out_...  102 us
    unnamed x3, local copies, waits for them, and re-layouts  5.01 us

profile of v1, /device:TPU:2, one launch (start us, length us, event | category | flops | bytes accessed | tf_op | source)
XLA Modules:
  0.0 110.5 jit_solution(14191510260334210957)
XLA Ops:
  1.3 0.5 broadcast_in_dim.18.climb_ref
  1.8 102.4 %band_step.1 = (f32[64,1024]{1,0:T(8,128)}, f32[64,1024]{1,0:T(8,128)}, f32[64,1000]{1,0:T(8,128)}, f32[8,128]{1,0:T(8,128)}) custom-call(f32[1,64,1024]{2,1,0:T(8,128)} %im_in.1, f32[1,64,1024]{2,1,0:T(8,128)} %im_mid.1, f32[1,64,1000]{2,1,0:T(8,128)} %im_out.1, f32[2,64,1024]{2,1,0:T(8,128)} %en_in.1, f32[2,64,1024]{2,1,0:T(8,128)} %en_mid.1, ...), custom_call_target="tpu_custom_call" | custom-call | flops 18320719872 | bytes 10000000 | tf_op jit(solution)/shard_map/band_step/pallas_call | solution.py:530
  104.2 1.3 %fusion = (f32[1,1]{1,0:T(1,128)}, f32[1,1]{1,0:T(1,128)}, f32[1,1]{1,0:T(1,128)}) fusion(f32[8,128]{1,0:T(8,128)} %get-tuple-element.13), kind=kLoop, calls=%fused_computation | loop fusion | bytes 24 | tf_op jit(solution)/shard_map/slice | solution.py:549
  105.5 1.7 %copy.20 = f32[1,64,1024]{2,1,0:T(8,128)} copy(f32[1,64,1024]{2,1,0:T(8,128)} %bitcast.10) | data formatting | bytes 524288
  107.2 1.7 %copy.21 = f32[1,64,1024]{2,1,0:T(8,128)} copy(f32[1,64,1024]{2,1,0:T(8,128)} %bitcast.9) | data formatting | bytes 524288
  108.8 1.7 %copy.22 = f32[1,64,1000]{2,1,0:T(8,128)} copy(f32[1,64,1000]{2,1,0:T(8,128)} %bitcast.8) | data formatting | bytes 512000

commit v2 on v1

--- a/solution.py
+++ b/solution.py
@@ -14,7 +14,7 @@
 F32 = jnp.float32
 BF16 = jnp.bfloat16
 SIDE = 4
-N_COPIES = 260
+N_COPIES = 280
 
 
 def mm(a, b):
@@ -50,12 +50,12 @@
 
 def kernel(
     dims,
-    im_in, im_mid, im_out, en_in, en_mid, en_out, pool_hbm, rows_ref, labs_ref, climb_ref,
+    im_in, im_mid, im_out, en_in, en_mid, en_out, pool_hbm, rows_hbm, labs_hbm, climb_hbm,
     up_in, up_mid, up_out, tab_ref,
     W, G, RA1, RAd, RAs, R1, RB1, RBd, RBs, gsh,
     own_in, own_mid, own_out, nb_in, nb_mid, nb_out, e_in, e_mid, e_out, AH, BH,
     pool, onehot, rcol, lcol, x, hid, slope, resid, dlog, dres, dpre,
-    mine, sums, chain_mine, chain_tab,
+    rows_ref, labs_ref, climb_ref, mine, sums, chain_tab,
     local_sem, send_sem, recv_sem,
 ):
     chain_n, batch, classes = dims
@@ -82,6 +82,11 @@
     def at_chain(step):
         return {"chain": lax.rem(ci + step, chain_n)}
 
+    barrier = pltpu.get_barrier_semaphore()
+    partners = [at_x(1), at_x(3), at_y(1), at_y(3), at_chain(1), at_chain(chain_n - 1)]
+    for device in partners:
+        pl.semaphore_signal(barrier, inc=1, device_id=device, device_id_type=pl.DeviceIdType.MESH)
+
     loads = []
 
     def load(src, dst):
@@ -93,15 +98,12 @@
     load(im_mid.at[0], own_mid)
     load(im_out.at[0], own_out)
     load(pool_hbm, pool)
+    load(rows_hbm, rows_ref)
+    load(labs_hbm, labs_ref)
+    load(climb_hbm, climb_ref)
     load(en_in, e_in)
     load(en_mid, e_mid)
     load(en_out, e_out)
-
-    barrier = pltpu.get_barrier_semaphore()
-    partners = [at_x(s) for s in (1, 2, 3)] + [at_y(s) for s in (1, 2, 3)]
-    partners += [at_chain(s) for s in range(1, chain_n)]
-    for device in partners:
-        pl.semaphore_signal(barrier, inc=1, device_id=device, device_id_type=pl.DeviceIdType.MESH)
 
     factors = (width ** (-0.5), hid.shape[1] ** (-0.5), width ** (-0.5))
     edge = classes // 128 * 128
@@ -121,12 +123,11 @@
     def far(h, d):
         return at_y(d) if h == 0 else at_x(d)
 
-    def w_near(m, h, step):
-        return W.at[m, yi, xs(step), h] if h == 0 else W.at[m, ys(step), xi, h]
-
-    def w_near_half(m, h, step, k):
-        r = pl.ds(16 * k, 16)
-        return W.at[m, yi, xs(step), h, r] if h == 0 else W.at[m, ys(step), xi, h, r]
+    def piece(m, h, far_step, near_step, k=None):
+        r = pl.ds(0, 32) if k is None else pl.ds(16 * k, 16)
+        if h == 0:
+            return W.at[m, ys(far_step), xs(near_step), h, r]
+        return W.at[m, ys(near_step), xs(far_step), h, r]
 
     def blocks(ref, m, h, step, k, cols=None):
         two = pl.ds(2 * k, 2)
@@ -136,43 +137,55 @@
         return ref.at[m, two, xs(step), 1, :, cols]
 
     BOTH = [(h, k) for h in (0, 1) for k in (0, 1)]
-    p1, p1f, p2a, p2b, p2f = {}, {}, {}, {}, {}
-    for m in range(3):
-        for h, k in BOTH:
-            src = w_near(m, h, 0)
-            p1[m, h, k] = cp.start(src, src, near(h, DIRS[k]))
+    ALL = pl.ds(0, 3)
+    near_one, near_fwd, own_far, own_fwd, far_one, far_fwd = {}, {}, {}, {}, {}, {}
+    for h, k in BOTH:
+        src = piece(ALL, h, 0, 0)
+        near_one[h, k] = cp.start(src, src, near(h, DIRS[k]))
+    for h, k in BOTH:
+        src = piece(ALL, h, 0, 0)
+        own_far[h, k] = cp.start(src, src, far(h, DIRS[k]))
 
     nb = []
     for own, buf in ((own_in, nb_in), (own_mid, nb_mid), (own_out, nb_out)):
         nb.append(cp.start(own, buf.at[0], at_chain(1)))
         nb.append(cp.start(own, buf.at[1], at_chain(chain_n - 1)))
 
-    def ag_near_forward(m):
-        for h, k in BOTH:
-            p1[m, h, k].wait_recv()
-            src = w_near_half(m, h, SIDE - DIRS[k], k)
-            p1f[m, h, k] = cp.start(src, src, near(h, DIRS[k]))
-
-    def ag_far_start(m):
-        for h, k in BOTH:
-            p1f[m, h, k].wait_recv()
-        for h, k in BOTH:
-            src = blocks(W, m, h, 0, k)
-            p2a[m, h, k] = cp.start(src, src, far(h, DIRS[k]))
-        for h, k in BOTH:
-            src = blocks(W, m, h, 0, 1 - k)
-            p2b[m, h, k] = cp.start(src, src, far(h, DIRS[k]))
-
-    def ag_far_forward(m):
-        for h, k in BOTH:
-            p2a[m, h, k].wait_recv()
-            src = blocks(W, m, h, SIDE - DIRS[k], k)
-            p2f[m, h, k] = cp.start(src, src, far(h, DIRS[k]))
+    def ag_near_forward():
+        for h, k in BOTH:
+            near_one[h, k].wait_recv()
+            src = piece(ALL, h, 0, SIDE - DIRS[k], k)
+            near_fwd[h, k] = cp.start(src, src, near(h, DIRS[k]))
+
+    def ag_far(m, steps):
+        for j in steps:
+            for h, k in BOTH:
+                src = piece(m, h, 0, j)
+                far_one[m, h, k, j] = cp.start(src, src, far(h, DIRS[k]))
+
+    def ag_own_forward():
+        for h, k in BOTH:
+            own_far[h, k].wait_recv()
+            src = piece(ALL, h, SIDE - DIRS[k], 0, k)
+            own_fwd[h, k] = cp.start(src, src, far(h, DIRS[k]))
+
+    def ag_near_end():
+        for h, k in BOTH:
+            near_fwd[h, k].wait_recv()
+
+    def ag_far_forward(m, steps):
+        for j in steps:
+            for h, k in BOTH:
+                far_one[m, h, k, j].wait_recv()
+                src = piece(m, h, SIDE - DIRS[k], j, k)
+                far_fwd[m, h, k, j] = cp.start(src, src, far(h, DIRS[k]))
 
     def ag_end(m):
         for h, k in BOTH:
-            p2b[m, h, k].wait_recv()
-            p2f[m, h, k].wait_recv()
+            if m == 0:
+                own_fwd[h, k].wait_recv()
+            for j in (1, 2, 3):
+                far_fwd[m, h, k, j].wait_recv()
 
     def weight(m):
         return W[m].reshape(width, width)
@@ -180,6 +193,10 @@
     def part(i):
         return pl.ds(i * half_rows, half_rows)
 
+    SIDES, ACROSS = (1, 3), (2,)
+
+    for c in loads[4:7]:
+        c.wait()
     for ref, col in ((rows_ref, rcol), (labs_ref, lcol)):
         for k in range(rows // 128):
             r = pl.ds(k * 128, 128)
@@ -196,13 +213,12 @@
 
     loads[3].wait()
     pick_rows(0)
-    ag_near_forward(0)
+    ag_near_forward()
+    ag_far(0, SIDES)
     pick_rows(1)
-    ag_near_forward(1)
-    ag_near_forward(2)
-    ag_far_start(0)
-
-    for c in loads[4:]:
+    ag_own_forward()
+
+    for c in loads[7:]:
         c.wait()
     for c in nb:
         c.wait_recv()
@@ -248,9 +264,14 @@
     x_peers = [at_x(s) for s in (1, 2, 3)]
     y_peers = [at_y(s) for s in (1, 2, 3)]
     early_x = exchange(0, pack(sq_b, sq_a, cross), xi, x_peers)
-    ag_far_forward(0)
-    ag_far_start(1)
+    ag_near_end()
+    ag_far(0, ACROSS)
+    ag_far(1, SIDES)
+    ag_far_forward(0, SIDES)
     early_y = exchange(1, collect(0, early_x, xi), yi, y_peers)
+    ag_far_forward(0, ACROSS)
+    ag_far(1, ACROSS)
+    ag_far(2, SIDES)
     early = jnp.sum(collect(1, early_y, yi), axis=1, keepdims=True)
     sq_behind = jnp.broadcast_to(early[0:1], (1, 128))
     sq_ahead = jnp.broadcast_to(early[1:2], (1, 128))
@@ -264,10 +285,22 @@
     )
     raw_len = jnp.sqrt(raw_sq + EPS)
     tau_sq = raw_sq / (raw_sq + EPS)
-    chain_mine[...] = pack(len_behind, len_ahead)
-    lengths = [
-        cp.start(chain_mine, chain_tab.at[ci], at_chain(s)) for s in range(1, chain_n)
-    ]
+    chain_tab[ci] = pack(len_behind, len_ahead)
+    up, down = {}, {}
+
+    def lengths(step):
+        if step > 1:
+            up[step - 1].wait_recv()
+        if step <= chain_n // 2:
+            src = chain_tab.at[lax.rem(ci + chain_n + 1 - step, chain_n)]
+            up[step] = cp.start(src, src, at_chain(1))
+        if 1 < step <= chain_n // 2:
+            down[step - 1].wait_recv()
+        if step < chain_n // 2:
+            src = chain_tab.at[lax.rem(ci + step - 1, chain_n)]
+            down[step] = cp.start(src, src, at_chain(chain_n - 1))
+
+    lengths(1)
 
     def forward_in(i):
         pre = mm(x[part(i), :], weight(0))
@@ -281,43 +314,38 @@
 
     norm = 1.0 / (batch * classes)
 
+    COLS = width // 2
+
+    def cols_of(c):
+        return pl.ds(c * COLS, COLS)
+
     def forward_out(i, energy):
-        logits = mm(resid[part(i), :], weight(2))
-        for c in range(width // 128):
-            hit = lcol[part(i), :] == lanes(c)
+        logits = mm(resid[...], W[2, :, :, :, :, cols_of(i)].reshape(width, COLS))
+        for c in range(COLS // 128):
+            at = i * COLS + c * 128
+            hit = lcol[...] == lanes(i * (COLS // 128) + c)
             err = logits[:, c * 128 : (c + 1) * 128] - jnp.where(hit, 1.0, 0.0)
             energy = energy + jnp.sum(err * err, axis=0, keepdims=True)
-            dlog[part(i), c * 128 : (c + 1) * 128] = (err * norm).astype(BF16)
+            dlog[:, at : at + 128] = (err * norm).astype(BF16)
         return energy
 
+    ag_far_forward(1, SIDES)
     ag_end(0)
     forward_in(0)
-    ag_far_forward(1)
-    ag_far_start(2)
+    ag_far_forward(1, ACROSS)
+    ag_far(2, ACROSS)
+    lengths(2)
     forward_in(1)
-    for c in lengths:
-        c.wait_recv()
-    chain_tab[ci] = chain_mine[...]
-    arc = jnp.zeros((1, 128), F32)
-    band = jnp.zeros((1, 128), F32)
-    for j in range(chain_n):
-        piece = chain_tab[j, 0:1]
-        arc = arc + jnp.where(j <= ci, piece, 0.0)
-        band = band + piece
-    band = band + chain_tab[chain_n - 1, 1:2]
+    ag_far_forward(2, SIDES)
+    lengths(3)
     ag_end(1)
     forward_mid(0)
+    ag_far_forward(2, ACROSS)
+    lengths(4)
     forward_mid(1)
-    ag_far_forward(2)
     ag_end(2)
-    energy = forward_out(0, jnp.zeros((1, 128), F32))
-    energy = forward_out(1, energy)
-
-    COLS = width // 2
+
     PIECES = [(m, c) for m in (2, 1, 0) for c in (0, 1)]
-
-    def cols_of(c):
-        return pl.ds(c * COLS, COLS)
 
     def grad(p, left, right):
         m, c = PIECES[p]
@@ -406,24 +434,30 @@
         d = mm_nt(dres[part(i), :], weight(1)) * slope[part(i), :]
         dpre[part(i), :] = d.astype(BF16)
 
+    energy = forward_out(0, jnp.zeros((1, 128), F32))
     grad(0, resid, dlog)
     rs_start(0)
+    energy = forward_out(1, energy)
     grad(1, resid, dlog)
     rs_start(1)
     back_resid(0)
     rs_far_sum(0)
+    lengths(5)
     back_resid(1)
     rs_far_sum(1)
+    lengths(6)
     grad(2, hid, dres)
     rs_start(2)
     grad(3, hid, dres)
     rs_start(3)
     back_pre(0)
     rs_far_sum(2)
+    lengths(7)
     back_pre(1)
     grad(4, x, dpre)
     rs_start(4)
     rs_far_sum(3)
+    lengths(8)
     grad(5, x, dpre)
     rs_start(5)
     rs_near_start(0)
@@ -431,6 +465,14 @@
     rs_near_start(1)
     rs_far_sum(5)
     rs_near_start(2)
+    lengths(9)
+    arc = jnp.zeros((1, 128), F32)
+    band = jnp.zeros((1, 128), F32)
+    for j in range(chain_n):
+        length = chain_tab[j, 0:1]
+        arc = arc + jnp.where(j <= ci, length, 0.0)
+        band = band + length
+    band = band + chain_tab[chain_n - 1, 1:2]
     rs_near_sum(0)
     rs_near_start(3)
     rs_near_sum(1)
@@ -456,7 +498,7 @@
     along = (g_ahead / len_ahead + g_behind / len_behind) / raw_len
     count = float(chain_n)
     goal = (ci + 1).astype(F32) / (count + 1.0) * band
-    climbing = climb_ref[:, 0:1] == 1
+    climbing = jnp.full((1, 128), climb_ref[0]) == 1
     coef = jnp.where(climbing, 2.0 * along, along + SPRING * (goal - arc) / band)
     force_sq = g_g - 2.0 * coef * along + coef * coef * tau_sq
     scale = band / (count + 1.0) / jnp.sqrt(force_sq + EPS)
@@ -470,6 +512,12 @@
     tab_ref[...] = pack(0.5 * norm * energy, arc / band, 0.5 * raw_len)
     for c in cp.all:
         c.wait_send()
+
+
+def hand_out(up_in, up_mid, up_out, tab, new_in, new_mid, new_out, energy, share, bend):
+    for up, new in ((up_in, new_in), (up_mid, new_mid), (up_out, new_out)):
+        new[0] = up[...]
+    energy[0], share[0], bend[0] = tab[0, 0], tab[1, 0], tab[2, 0]
 
 
 def on_device(
@@ -518,15 +566,16 @@
         vm((rows, width), BF16),
         vm((rows, width), BF16),
         vm((rows, width), BF16),
+        vm((1, rows), jnp.int32),
+        vm((1, rows), jnp.int32),
+        pltpu.SMEM((1,), jnp.int32),
         vm((4, 8, 128), F32),
         vm((4, SIDE, 8, 128), F32),
-        vm((8, 128), F32),
         vm((chain_n, 8, 128), F32),
-        pltpu.SemaphoreType.DMA((7,)),
+        pltpu.SemaphoreType.DMA((10,)),
         pltpu.SemaphoreType.DMA((N_COPIES,)),
         pltpu.SemaphoreType.DMA((N_COPIES,)),
     ]
-    climb = jnp.broadcast_to(climbing[:, None], (1, 128))
     up_in, up_mid, up_out, tab = pl.pallas_call(
         functools.partial(kernel, (chain_n, batch, classes)),
         out_shape=(
@@ -535,18 +584,33 @@
             jax.ShapeDtypeStruct((shard, classes), F32),
             jax.ShapeDtypeStruct((8, 128), F32),
         ),
-        in_specs=[any_spec] * 7 + [vmem_spec] * 3,
+        in_specs=[any_spec] * 9 + [pl.BlockSpec(memory_space=pltpu.HBM)],
         out_specs=(vmem_spec,) * 4,
         scratch_shapes=scratch,
         compiler_params=pltpu.CompilerParams(
-            collective_id=0, has_side_effects=True, vmem_limit_bytes=60 * 2**20
+            collective_id=0, has_side_effects=True, vmem_limit_bytes=56 * 2**20
         ),
         cost_estimate=pl.CostEstimate(
             flops=2 * rows * width * (8 * width + pool_rows), bytes_accessed=10**7, transcendentals=10**6
         ),
         name="band_step",
-    )(images_in, images_mid, images_out, ends_in, ends_mid, ends_out, data_pool, batch_rows, labels, climb)
-    return (up_in[None], up_mid[None], up_out[None], tab[0, 0:1], tab[1, 0:1], tab[2, 0:1])
+    )(images_in, images_mid, images_out, ends_in, ends_mid, ends_out, data_pool, batch_rows, labels, climbing)
+    scalar = jax.ShapeDtypeStruct((1,), F32)
+    smem_spec = pl.BlockSpec(memory_space=pltpu.SMEM)
+    return pl.pallas_call(
+        hand_out,
+        out_shape=(
+            jax.ShapeDtypeStruct(images_in.shape, F32),
+            jax.ShapeDtypeStruct(images_mid.shape, F32),
+            jax.ShapeDtypeStruct(images_out.shape, F32),
+            scalar,
+            scalar,
+            scalar,
+        ),
+        in_specs=[vmem_spec] * 3 + [smem_spec],
+        out_specs=(vmem_spec,) * 3 + (smem_spec,) * 3,
+        name="hand_out",
+    )(up_in, up_mid, up_out, tab)
 
 
 def solution(mesh):

time: 111 us -> 99.1 us (0.89)
  local copies, waits for them, and re-layouts: 6.83 us -> 0 us
  Pallas kernels: 102 us -> 97.5 us
    pallas_call x1, Pallas kernels: 102 us -> 95.5 us  [on_device(): pl.pallas_call(functools.partial(kernel, (chain_n, batch, classes)), out_...]
    unnamed x3 -> x0, local copies, waits for them, and re-layouts: 5.01 us -> none
    pallas_call x0 -> x1, Pallas kernels: none -> 2.03 us  [on_device(): pl.pallas_call(hand_out, out_shape=(jax.ShapeDtypeStruct(images_in.shape,...]
    slice x1 -> x0, local copies, waits for them, and re-layouts: 1.31 us -> none  [on_device(): tab[2, 0:1]]
where the time goes in v2:
time: 99.1 us; the launch traced here: 98.9 us
  Pallas kernels  97.5 us (98%)
  between operations  1.45 us (1%)
    pallas_call x1, Pallas kernels, on_device(): pl.pallas_call(functools.partial(kernel, (chain_n, batch, classes)), out_...  95.5 us
    pallas_call x1, Pallas kernels, on_device(): pl.pallas_call(hand_out, out_shape=(jax.ShapeDtypeStruct(images_in.shape,...  2.03 us

profile of v2, /device:TPU:2, one launch (start us, length us, event | category | flops | bytes accessed | tf_op | source)
XLA Modules:
  0.0 98.9 jit_solution(11883842464271922005)
XLA Ops:
  1.3 95.5 %band_step.1 = (f32[64,1024]{1,0:T(8,128)}, f32[64,1024]{1,0:T(8,128)}, f32[64,1000]{1,0:T(8,128)}, f32[8,128]{1,0:T(8,128)}) custom-call(f32[1,64,1024]{2,1,0:T(8,128)} %im_in.1, f32[1,64,1024]{2,1,0:T(8,128)} %im_mid.1, f32[1,64,1000]{2,1,0:T(8,128)} %im_out.1, f32[2,64,1024]{2,1,0:T(8,128)} %en_in.1, f32[2,64,1024]{2,1,0:T(8,128)} %en_mid.1, ...), custom_call_target="tpu_custom_call" | custom-call | flops 18320719872 | bytes 10000000 | tf_op jit(solution)/shard_map/band_step/pallas_call | solution.py:579
  96.8 2.0 %hand_out.1 = (f32[1,64,1024]{2,1,0:T(8,128)}, f32[1,64,1024]{2,1,0:T(8,128)}, f32[1,64,1000]{2,1,0:T(8,128)}, f32[1]{0:T(128)}, f32[1]{0:T(128)}, /*index=5*/f32[1]{0:T(128)}) custom-call(f32[64,1024]{1,0:T(8,128)} %get-tuple-element.10.up_in, f32[64,1024]{1,0:T(8,128)} %get-tuple-element.11.up_mid, f32[64,1000]{1,0:T(8,128)} %get-tuple-element.12.up_out, ...), custom_call_target="tpu_custom_call" | custom-call | tf_op jit(solution)/shard_map/hand_out/pallas_call | solution.py:600

commit v3 on v2

--- a/solution.py
+++ b/solution.py
@@ -14,7 +14,7 @@
 F32 = jnp.float32
 BF16 = jnp.bfloat16
 SIDE = 4
-N_COPIES = 280
+N_COPIES = 64
 
 
 def mm(a, b):
@@ -27,25 +27,42 @@
 
 def mm_tn(a, b):
     return lax.dot_general(a, b, (((0,), (0,)), ((), ())), preferred_element_type=F32)
+
+
+class Group:
+    def __init__(self, copies, whole):
+        i = len(copies.all)
+        self.sems = (copies.send.at[i], copies.recv.at[i])
+        self.whole = whole
+        copies.all.append(self)
+
+    def _copy(self, src, dst, device):
+        return pltpu.make_async_remote_copy(
+            src_ref=src,
+            dst_ref=dst,
+            send_sem=self.sems[0],
+            recv_sem=self.sems[1],
+            device_id=device,
+            device_id_type=pl.DeviceIdType.MESH,
+        )
+
+    def start(self, src, dst, device):
+        self.device = device
+        self._copy(src, dst, device).start()
+
+    def wait_recv(self):
+        self._copy(self.whole, self.whole, self.device).wait_recv()
+
+    def wait_send(self):
+        self._copy(self.whole, self.whole, self.device).wait_send()
 
 
 class Copies:
     def __init__(self, send, recv):
         self.send, self.recv, self.all = send, recv, []
 
-    def start(self, src, dst, device):
-        i = len(self.all)
-        copy = pltpu.make_async_remote_copy(
-            src_ref=src,
-            dst_ref=dst,
-            send_sem=self.send.at[i],
-            recv_sem=self.recv.at[i],
-            device_id=device,
-            device_id_type=pl.DeviceIdType.MESH,
-        )
-        copy.start()
-        self.all.append(copy)
-        return copy
+    def group(self, whole):
+        return Group(self, whole)
 
 
 def kernel(
@@ -55,7 +72,7 @@
     W, G, RA1, RAd, RAs, R1, RB1, RBd, RBs, gsh,
     own_in, own_mid, own_out, nb_in, nb_mid, nb_out, e_in, e_mid, e_out, AH, BH,
     pool, onehot, rcol, lcol, x, hid, slope, resid, dlog, dres, dpre,
-    rows_ref, labs_ref, climb_ref, mine, sums, chain_tab,
+    rows_ref, labs_ref, climb_ref, sums, chain_tab, out_in, out_mid, out_out, out_tab,
     local_sem, send_sem, recv_sem,
 ):
     chain_n, batch, classes = dims
@@ -138,54 +155,60 @@
 
     BOTH = [(h, k) for h in (0, 1) for k in (0, 1)]
     ALL = pl.ds(0, 3)
-    near_one, near_fwd, own_far, own_fwd, far_one, far_fwd = {}, {}, {}, {}, {}, {}
+    near_one = cp.group(W.at[ALL, 0, :, 0])
+    own_far = cp.group(W.at[ALL, 0, :, 0])
+    far_one, far_fwd = {}, {}
     for h, k in BOTH:
         src = piece(ALL, h, 0, 0)
-        near_one[h, k] = cp.start(src, src, near(h, DIRS[k]))
+        near_one.start(src, src, near(h, DIRS[k]))
     for h, k in BOTH:
         src = piece(ALL, h, 0, 0)
-        own_far[h, k] = cp.start(src, src, far(h, DIRS[k]))
+        own_far.start(src, src, far(h, DIRS[k]))
 
     nb = []
     for own, buf in ((own_in, nb_in), (own_mid, nb_mid), (own_out, nb_out)):
-        nb.append(cp.start(own, buf.at[0], at_chain(1)))
-        nb.append(cp.start(own, buf.at[1], at_chain(chain_n - 1)))
+        nb.append(cp.group(buf))
+        nb[-1].start(own, buf.at[0], at_chain(1))
+        nb[-1].start(own, buf.at[1], at_chain(chain_n - 1))
+
+    near_fwd = cp.group(W.at[ALL, 0, pl.ds(0, 2), 0])
+    own_fwd = cp.group(W.at[ALL, 0, pl.ds(0, 2), 0])
 
     def ag_near_forward():
+        near_one.wait_recv()
         for h, k in BOTH:
-            near_one[h, k].wait_recv()
             src = piece(ALL, h, 0, SIDE - DIRS[k], k)
-            near_fwd[h, k] = cp.start(src, src, near(h, DIRS[k]))
+            near_fwd.start(src, src, near(h, DIRS[k]))
 
     def ag_far(m, steps):
+        far_one[m, steps] = cp.group(W.at[m, pl.ds(0, len(steps)), :, 0])
         for j in steps:
             for h, k in BOTH:
                 src = piece(m, h, 0, j)
-                far_one[m, h, k, j] = cp.start(src, src, far(h, DIRS[k]))
+                far_one[m, steps].start(src, src, far(h, DIRS[k]))
 
     def ag_own_forward():
+        own_far.wait_recv()
         for h, k in BOTH:
-            own_far[h, k].wait_recv()
             src = piece(ALL, h, SIDE - DIRS[k], 0, k)
-            own_fwd[h, k] = cp.start(src, src, far(h, DIRS[k]))
+            own_fwd.start(src, src, far(h, DIRS[k]))
 
     def ag_near_end():
-        for h, k in BOTH:
-            near_fwd[h, k].wait_recv()
+        near_fwd.wait_recv()
 
     def ag_far_forward(m, steps):
+        far_one[m, steps].wait_recv()
+        far_fwd[m, steps] = cp.group(W.at[m, 0, pl.ds(0, 2 * len(steps)), 0])
         for j in steps:
             for h, k in BOTH:
-                far_one[m, h, k, j].wait_recv()
                 src = piece(m, h, SIDE - DIRS[k], j, k)
-                far_fwd[m, h, k, j] = cp.start(src, src, far(h, DIRS[k]))
+                far_fwd[m, steps].start(src, src, far(h, DIRS[k]))
 
     def ag_end(m):
-        for h, k in BOTH:
-            if m == 0:
-                own_fwd[h, k].wait_recv()
-            for j in (1, 2, 3):
-                far_fwd[m, h, k, j].wait_recv()
+        if m == 0:
+            own_fwd.wait_recv()
+        far_fwd[m, SIDES].wait_recv()
+        far_fwd[m, ACROSS].wait_recv()
 
     def weight(m):
         return W[m].reshape(width, width)
@@ -245,34 +268,73 @@
         sq_a, sq_b, cross = sq_a + fold(a * a), sq_b + fold(z * z), cross + fold(a * z)
 
     def pack(*values):
-        zero = jnp.zeros((8 - len(values), 128), F32)
-        return jnp.concatenate([*values, zero], axis=0)
-
-    def exchange(slot, tile, index, peers):
-        mine[slot] = tile
-        return [cp.start(mine.at[slot], sums.at[slot, index], device) for device in peers]
-
-    def collect(slot, copies, index):
-        for c in copies:
-            c.wait_recv()
-        sums[slot, index] = mine[slot]
+        zero = jnp.zeros((4 - len(values), 128), F32)
+        return jnp.concatenate([*values, zero], axis=0) if len(values) < 4 else jnp.concatenate(values, axis=0)
+
+    me = yi * SIDE + xi
+    others = [(i, j) for i in range(SIDE) for j in range(SIDE) if i or j]
+
+    def exchange(slot, tile):
+        sums[slot, me] = tile
+        src = sums.at[slot, me]
+        g = cp.group(sums.at[slot, pl.ds(0, len(others))])
+        for i, j in others:
+            g.start(src, src, {**at_y(i), **at_x(j)})
+        return g
+
+    def collect(slot, copies):
+        copies.wait_recv()
         out = sums[slot, 0]
-        for k in range(1, SIDE):
+        for k in range(1, SIDE * SIDE):
             out = out + sums[slot, k]
-        return out
-
-    x_peers = [at_x(s) for s in (1, 2, 3)]
-    y_peers = [at_y(s) for s in (1, 2, 3)]
-    early_x = exchange(0, pack(sq_b, sq_a, cross), xi, x_peers)
+        return jnp.sum(out, axis=1, keepdims=True)
+
     ag_near_end()
     ag_far(0, ACROSS)
     ag_far(1, SIDES)
     ag_far_forward(0, SIDES)
-    early_y = exchange(1, collect(0, early_x, xi), yi, y_peers)
     ag_far_forward(0, ACROSS)
     ag_far(1, ACROSS)
     ag_far(2, SIDES)
-    early = jnp.sum(collect(1, early_y, yi), axis=1, keepdims=True)
+    early = exchange(0, pack(sq_b, sq_a, cross))
+    def forward_in(i):
+        pre = mm(x[part(i), :], weight(0))
+        sig = jax.nn.sigmoid(pre)
+        hid[part(i), :] = (pre * sig).astype(BF16)
+        slope[part(i), :] = sig * (1.0 + pre * (1.0 - sig))
+
+    def forward_mid(i):
+        r = x[part(i), :].astype(F32) + mm(hid[part(i), :], weight(1))
+        resid[part(i), :] = r.astype(BF16)
+
+    norm = 1.0 / (batch * classes)
+
+    HALF, QUARTER = width // 2, width // 4
+    PIECES = [
+        (2, 0, QUARTER), (2, QUARTER, QUARTER), (2, HALF, HALF),
+        (1, 0, HALF), (1, HALF, HALF), (0, 0, HALF), (0, HALF, HALF),
+    ]
+
+    def cols_of(p):
+        return pl.ds(PIECES[p][1], PIECES[p][2])
+
+    def forward_out(p, energy):
+        _, first_col, n = PIECES[p]
+        logits = mm(resid[...], W[2, :, :, :, :, cols_of(p)].reshape(width, n))
+        for c in range(n // 128):
+            at = first_col + c * 128
+            hit = lcol[...] == lanes(at // 128)
+            err = logits[:, c * 128 : (c + 1) * 128] - jnp.where(hit, 1.0, 0.0)
+            energy = energy + jnp.sum(err * err, axis=0, keepdims=True)
+            dlog[:, at : at + 128] = (err * norm).astype(BF16)
+        return energy
+
+    ag_far_forward(1, SIDES)
+    ag_end(0)
+    forward_in(0)
+    ag_far_forward(1, ACROSS)
+    ag_far(2, ACROSS)
+    early = collect(0, early)
     sq_behind = jnp.broadcast_to(early[0:1], (1, 128))
     sq_ahead = jnp.broadcast_to(early[1:2], (1, 128))
     cross = jnp.broadcast_to(early[2:3], (1, 128))
@@ -293,129 +355,92 @@
             up[step - 1].wait_recv()
         if step <= chain_n // 2:
             src = chain_tab.at[lax.rem(ci + chain_n + 1 - step, chain_n)]
-            up[step] = cp.start(src, src, at_chain(1))
+            up[step] = cp.group(src)
+            up[step].start(src, src, at_chain(1))
         if 1 < step <= chain_n // 2:
             down[step - 1].wait_recv()
         if step < chain_n // 2:
             src = chain_tab.at[lax.rem(ci + step - 1, chain_n)]
-            down[step] = cp.start(src, src, at_chain(chain_n - 1))
+            down[step] = cp.group(src)
+            down[step].start(src, src, at_chain(chain_n - 1))
 
     lengths(1)
 
-    def forward_in(i):
-        pre = mm(x[part(i), :], weight(0))
-        sig = jax.nn.sigmoid(pre)
-        hid[part(i), :] = (pre * sig).astype(BF16)
-        slope[part(i), :] = sig * (1.0 + pre * (1.0 - sig))
-
-    def forward_mid(i):
-        r = x[part(i), :].astype(F32) + mm(hid[part(i), :], weight(1))
-        resid[part(i), :] = r.astype(BF16)
-
-    norm = 1.0 / (batch * classes)
-
-    COLS = width // 2
-
-    def cols_of(c):
-        return pl.ds(c * COLS, COLS)
-
-    def forward_out(i, energy):
-        logits = mm(resid[...], W[2, :, :, :, :, cols_of(i)].reshape(width, COLS))
-        for c in range(COLS // 128):
-            at = i * COLS + c * 128
-            hit = lcol[...] == lanes(i * (COLS // 128) + c)
-            err = logits[:, c * 128 : (c + 1) * 128] - jnp.where(hit, 1.0, 0.0)
-            energy = energy + jnp.sum(err * err, axis=0, keepdims=True)
-            dlog[:, at : at + 128] = (err * norm).astype(BF16)
-        return energy
-
-    ag_far_forward(1, SIDES)
-    ag_end(0)
-    forward_in(0)
-    ag_far_forward(1, ACROSS)
-    ag_far(2, ACROSS)
-    lengths(2)
     forward_in(1)
     ag_far_forward(2, SIDES)
-    lengths(3)
+    lengths(2)
     ag_end(1)
     forward_mid(0)
     ag_far_forward(2, ACROSS)
+    lengths(3)
+    forward_mid(1)
     lengths(4)
-    forward_mid(1)
     ag_end(2)
 
-    PIECES = [(m, c) for m in (2, 1, 0) for c in (0, 1)]
 
     def grad(p, left, right):
-        m, c = PIECES[p]
-        g = mm_tn(left[...], right[:, cols_of(c)]).astype(BF16)
-        G[m, :, :, :, :, cols_of(c)] = g.reshape(SIDE, SIDE, 2, 32, COLS)
-
-    a1, ad, a_s, b1, bd, bs = {}, {}, {}, {}, {}, {}
+        m, _, n = PIECES[p]
+        g = mm_tn(left[...], right[:, cols_of(p)]).astype(BF16)
+        G[m, :, :, :, :, cols_of(p)] = g.reshape(SIDE, SIDE, 2, 32, n)
+
+    a1, a2, b1, b2 = {}, {}, {}, {}
 
     def rs_start(p):
-        m, c = PIECES[p]
-        q = cols_of(c)
+        m, q = PIECES[p][0], cols_of(p)
+        a1[p] = cp.group(G.at[m, pl.ds(0, 2), :, 0, :, q])
+        a2[p] = cp.group(G.at[m, :, :, 0, :, q])
         for h, k in BOTH:
             dst = RA1.at[m, h, k, :, :, q]
-            a1[p, h, k] = cp.start(blocks(G, m, h, 2, k, q), dst, far(h, DIRS[k]))
+            a1[p].start(blocks(G, m, h, 2, k, q), dst, far(h, DIRS[k]))
         for h, k in BOTH:
             dst = RAd.at[m, h, k, :, :, q]
-            src = blocks(G, m, h, DIRS[k], 1 - k, q)
-            ad[p, h, k] = cp.start(src, dst, far(h, DIRS[k]))
+            a2[p].start(blocks(G, m, h, DIRS[k], 1 - k, q), dst, far(h, DIRS[k]))
 
     def rs_far_sum(p):
-        m, c = PIECES[p]
-        q = cols_of(c)
+        m, q = PIECES[p][0], cols_of(p)
+        a1[p].wait_recv()
         for h, k in BOTH:
-            a1[p, h, k].wait_recv()
             mid = RA1.at[m, h, k, :, :, q]
             own_g = blocks(G, m, h, DIRS[k], k, q)
             mid[...] = (mid[...].astype(F32) + own_g[...].astype(F32)).astype(BF16)
-            a_s[p, h, k] = cp.start(mid, RAs.at[m, h, k, :, :, q], far(h, DIRS[k]))
+            a2[p].start(mid, RAs.at[m, h, k, :, :, q], far(h, DIRS[k]))
 
     def rs_near_start(p):
-        m, c = PIECES[p]
-        q = cols_of(c)
+        m, q = PIECES[p][0], cols_of(p)
+        a2[p].wait_recv()
+        b1[p] = cp.group(G.at[m, 0, pl.ds(0, 2), 0, :, q])
+        b2[p] = cp.group(G.at[m, 0, :, 0, :, q])
         for h in (0, 1):
-            for k in (0, 1):
-                ad[p, h, k].wait_recv()
-                a_s[p, h, k].wait_recv()
             for k in (0, 1):
                 total = blocks(G, m, h, 0, k, q)[...].astype(F32)
                 total = total + RAs[m, h, k, :, :, q].astype(F32)
                 total = total + RAd[m, h, 1 - k, :, :, q].astype(F32)
                 R1[m, h, pl.ds(2 * k, 2), :, q] = total.astype(BF16)
+            step = ys if h else xs
             for k in (0, 1):
-                step = ys if h else xs
                 src = R1.at[m, h, step(2), pl.ds(16 * k, 16), q]
-                b1[p, h, k] = cp.start(src, RB1.at[m, h, k, :, q], near(h, DIRS[k]))
+                b1[p].start(src, RB1.at[m, h, k, :, q], near(h, DIRS[k]))
             for k in (0, 1):
                 src = R1.at[m, h, step(DIRS[k]), pl.ds(16 * (1 - k), 16), q]
-                bd[p, h, k] = cp.start(src, RBd.at[m, h, k, :, q], near(h, DIRS[k]))
+                b2[p].start(src, RBd.at[m, h, k, :, q], near(h, DIRS[k]))
 
     def rs_near_sum(p):
-        m, c = PIECES[p]
-        q = cols_of(c)
+        m, q = PIECES[p][0], cols_of(p)
+        b1[p].wait_recv()
         for h, k in BOTH:
             step = ys if h else xs
-            b1[p, h, k].wait_recv()
             mid = RB1.at[m, h, k, :, q]
             own_r = R1[m, h, step(DIRS[k]), pl.ds(16 * k, 16), q]
             mid[...] = (mid[...].astype(F32) + own_r.astype(F32)).astype(BF16)
-            bs[p, h, k] = cp.start(mid, RBs.at[m, h, k, :, q], near(h, DIRS[k]))
+            b2[p].start(mid, RBs.at[m, h, k, :, q], near(h, DIRS[k]))
 
     dots = [jnp.zeros((1, 128), F32)] * 3
 
     def rs_end(p):
-        m, c = PIECES[p]
-        q = cols_of(c)
+        m, q = PIECES[p][0], cols_of(p)
+        b2[p].wait_recv()
         for h in (0, 1):
             step = ys if h else xs
-            for k in (0, 1):
-                bd[p, h, k].wait_recv()
-                bs[p, h, k].wait_recv()
             for k in (0, 1):
                 total = R1[m, h, step(0), pl.ds(16 * k, 16), q].astype(F32)
                 total = total + RBs[m, h, k, :, q].astype(F32)
@@ -440,31 +465,36 @@
     energy = forward_out(1, energy)
     grad(1, resid, dlog)
     rs_start(1)
+    energy = forward_out(2, energy)
+    rs_far_sum(0)
+    grad(2, resid, dlog)
+    rs_start(2)
+    rs_far_sum(1)
+    lengths(5)
     back_resid(0)
-    rs_far_sum(0)
-    lengths(5)
     back_resid(1)
-    rs_far_sum(1)
+    rs_far_sum(2)
     lengths(6)
-    grad(2, hid, dres)
-    rs_start(2)
     grad(3, hid, dres)
     rs_start(3)
+    grad(4, hid, dres)
+    rs_start(4)
     back_pre(0)
-    rs_far_sum(2)
+    rs_far_sum(3)
     lengths(7)
     back_pre(1)
-    grad(4, x, dpre)
-    rs_start(4)
-    rs_far_sum(3)
-    lengths(8)
     grad(5, x, dpre)
     rs_start(5)
+    rs_far_sum(4)
+    lengths(8)
+    grad(6, x, dpre)
+    rs_start(6)
     rs_near_start(0)
-    rs_far_sum(4)
     rs_near_start(1)
     rs_far_sum(5)
     rs_near_start(2)
+    rs_far_sum(6)
+    rs_near_start(3)
     lengths(9)
     arc = jnp.zeros((1, 128), F32)
     band = jnp.zeros((1, 128), F32)
@@ -474,24 +504,24 @@
         band = band + length
     band = band + chain_tab[chain_n - 1, 1:2]
     rs_near_sum(0)
-    rs_near_start(3)
     rs_near_sum(1)
     rs_near_start(4)
     rs_near_sum(2)
     rs_near_start(5)
     rs_near_sum(3)
+    rs_near_start(6)
+    rs_near_sum(4)
     rs_end(0)
     rs_end(1)
-    rs_near_sum(4)
     rs_end(2)
     rs_near_sum(5)
     rs_end(3)
+    rs_near_sum(6)
     rs_end(4)
     rs_end(5)
-
-    late_x = exchange(2, pack(*dots, energy), xi, x_peers)
-    late_y = exchange(3, collect(2, late_x, xi), yi, y_peers)
-    late = jnp.sum(collect(3, late_y, yi), axis=1, keepdims=True)
+    rs_end(6)
+
+    late = collect(1, exchange(1, pack(*dots, energy)))
     g_ahead, g_behind, g_g, energy = (
         jnp.broadcast_to(late[k : k + 1], (1, 128)) for k in range(4)
     )
@@ -505,13 +535,24 @@
     wa = (scale * coef / (len_ahead * raw_len))[:, 0:1]
     wb = (scale * coef / (len_behind * raw_len))[:, 0:1]
     scale = scale[:, 0:1]
-    for m, up in enumerate((up_in, up_mid, up_out)):
+    saves = []
+
+    def save(src, dst):
+        c = pltpu.make_async_copy(src, dst, local_sem.at[10 + len(saves)])
+        c.start()
+        saves.append(c)
+
+    out_tab[...] = pack(0.5 * norm * energy, arc / band, 0.5 * raw_len)
+    save(out_tab, tab_ref)
+    for m, (up, dst) in enumerate(((out_in, up_in), (out_mid, up_mid), (out_out, up_out))):
         n = up.shape[1]
         u = wa * AH[m, :, :n] + wb * BH[m, :, :n] - scale * gsh[m, :, :n]
         up[...] = own[m][...] + u
-    tab_ref[...] = pack(0.5 * norm * energy, arc / band, 0.5 * raw_len)
+        save(up, dst)
     for c in cp.all:
         c.wait_send()
+    for c in saves:
+        c.wait()
 
 
 def hand_out(up_in, up_mid, up_out, tab, new_in, new_mid, new_out, energy, share, bend):
@@ -569,10 +610,13 @@
         vm((1, rows), jnp.int32),
         vm((1, rows), jnp.int32),
         pltpu.SMEM((1,), jnp.int32),
-        vm((4, 8, 128), F32),
-        vm((4, SIDE, 8, 128), F32),
-        vm((chain_n, 8, 128), F32),
-        pltpu.SemaphoreType.DMA((10,)),
+        vm((2, SIDE * SIDE, 4, 128), F32),
+        vm((chain_n, 4, 128), F32),
+        vm((shard, width), F32),
+        vm((shard, width), F32),
+        vm((shard, classes), F32),
+        vm((4, 128), F32),
+        pltpu.SemaphoreType.DMA((14,)),
         pltpu.SemaphoreType.DMA((N_COPIES,)),
         pltpu.SemaphoreType.DMA((N_COPIES,)),
     ]
@@ -582,10 +626,10 @@
             jax.ShapeDtypeStruct((shard, hidden_units), F32),
             jax.ShapeDtypeStruct((shard, width), F32),
             jax.ShapeDtypeStruct((shard, classes), F32),
-            jax.ShapeDtypeStruct((8, 128), F32),
+            jax.ShapeDtypeStruct((4, 128), F32),
         ),
         in_specs=[any_spec] * 9 + [pl.BlockSpec(memory_space=pltpu.HBM)],
-        out_specs=(vmem_spec,) * 4,
+        out_specs=(any_spec,) * 4,
         scratch_shapes=scratch,
         compiler_params=pltpu.CompilerParams(
             collective_id=0, has_side_effects=True, vmem_limit_bytes=56 * 2**20

time: 99.1 us -> 96.6 us (0.975)
  Pallas kernels: 97.5 us -> 95 us
    pallas_call x1, Pallas kernels: 95.5 us -> 93 us  [on_device(): pl.pallas_call(functools.partial(kernel, (chain_n, batch, classes)), out_...]
where the time goes in v3:
time: 96.6 us; the launch traced here: 96.5 us
  Pallas kernels  95 us (98%)
  between operations  1.45 us (2%)
    pallas_call x1, Pallas kernels, on_device(): pl.pallas_call(functools.partial(kernel, (chain_n, batch, classes)), out_...  93 us
    pallas_call x1, Pallas kernels, on_device(): pl.pallas_call(hand_out, out_shape=(jax.ShapeDtypeStruct(images_in.shape,...  2.03 us

profile of v3, /device:TPU:2, one launch (start us, length us, event | category | flops | bytes accessed | tf_op | source)
XLA Modules:
  0.0 96.5 jit_solution(1500444683011582512)
XLA Ops:
  1.3 93.0 %band_step.1 = (f32[64,1024]{1,0:T(8,128)}, f32[64,1024]{1,0:T(8,128)}, f32[64,1000]{1,0:T(8,128)}, f32[4,128]{1,0:T(4,128)}) custom-call(f32[1,64,1024]{2,1,0:T(8,128)} %im_in.1, f32[1,64,1024]{2,1,0:T(8,128)} %im_mid.1, f32[1,64,1000]{2,1,0:T(8,128)} %im_out.1, f32[2,64,1024]{2,1,0:T(8,128)} %en_in.1, f32[2,64,1024]{2,1,0:T(8,128)} %en_mid.1, ...), custom_call_target="tpu_custom_call" | custom-call | flops 18320719872 | bytes 10000000 | tf_op jit(solution)/shard_map/band_step/pallas_call | solution.py:623
  94.3 2.0 %hand_out.1 = (f32[1,64,1024]{2,1,0:T(8,128)}, f32[1,64,1024]{2,1,0:T(8,128)}, f32[1,64,1000]{2,1,0:T(8,128)}, f32[1]{0:T(128)}, f32[1]{0:T(128)}, /*index=5*/f32[1]{0:T(128)}) custom-call(f32[64,1024]{1,0:T(8,128)} %get-tuple-element.10.up_in, f32[64,1024]{1,0:T(8,128)} %get-tuple-element.11.up_mid, f32[64,1000]{1,0:T(8,128)} %get-tuple-element.12.up_out, ...), custom_call_target="tpu_custom_call" | custom-call | tf_op jit(solution)/shard_map/hand_out/pallas_call | solution.py:644

commit v4 on v3

--- a/solution.py
+++ b/solution.py
@@ -293,10 +293,10 @@
     ag_far(0, ACROSS)
     ag_far(1, SIDES)
     ag_far_forward(0, SIDES)
+    ag_far(1, ACROSS)
     ag_far_forward(0, ACROSS)
-    ag_far(1, ACROSS)
     ag_far(2, SIDES)
-    early = exchange(0, pack(sq_b, sq_a, cross))
+    ag_far(2, ACROSS)
     def forward_in(i):
         pre = mm(x[part(i), :], weight(0))
         sig = jax.nn.sigmoid(pre)
@@ -329,52 +329,17 @@
             dlog[:, at : at + 128] = (err * norm).astype(BF16)
         return energy
 
-    ag_far_forward(1, SIDES)
     ag_end(0)
     forward_in(0)
+    ag_far_forward(1, SIDES)
     ag_far_forward(1, ACROSS)
-    ag_far(2, ACROSS)
-    early = collect(0, early)
-    sq_behind = jnp.broadcast_to(early[0:1], (1, 128))
-    sq_ahead = jnp.broadcast_to(early[1:2], (1, 128))
-    cross = jnp.broadcast_to(early[2:3], (1, 128))
-    len_ahead = jnp.sqrt(sq_ahead + EPS)
-    len_behind = jnp.sqrt(sq_behind + EPS)
-    raw_sq = (
-        sq_ahead / (len_ahead * len_ahead)
-        + sq_behind / (len_behind * len_behind)
-        + 2.0 * cross / (len_ahead * len_behind)
-    )
-    raw_len = jnp.sqrt(raw_sq + EPS)
-    tau_sq = raw_sq / (raw_sq + EPS)
-    chain_tab[ci] = pack(len_behind, len_ahead)
-    up, down = {}, {}
-
-    def lengths(step):
-        if step > 1:
-            up[step - 1].wait_recv()
-        if step <= chain_n // 2:
-            src = chain_tab.at[lax.rem(ci + chain_n + 1 - step, chain_n)]
-            up[step] = cp.group(src)
-            up[step].start(src, src, at_chain(1))
-        if 1 < step <= chain_n // 2:
-            down[step - 1].wait_recv()
-        if step < chain_n // 2:
-            src = chain_tab.at[lax.rem(ci + step - 1, chain_n)]
-            down[step] = cp.group(src)
-            down[step].start(src, src, at_chain(chain_n - 1))
-
-    lengths(1)
-
     forward_in(1)
     ag_far_forward(2, SIDES)
-    lengths(2)
+    ag_far_forward(2, ACROSS)
     ag_end(1)
     forward_mid(0)
-    ag_far_forward(2, ACROSS)
-    lengths(3)
     forward_mid(1)
-    lengths(4)
+    early = exchange(0, pack(sq_b, sq_a, cross))
     ag_end(2)
 
 
@@ -470,31 +435,70 @@
     grad(2, resid, dlog)
     rs_start(2)
     rs_far_sum(1)
-    lengths(5)
+    early = collect(0, early)
+    sq_behind = jnp.broadcast_to(early[0:1], (1, 128))
+    sq_ahead = jnp.broadcast_to(early[1:2], (1, 128))
+    cross = jnp.broadcast_to(early[2:3], (1, 128))
+    len_ahead = jnp.sqrt(sq_ahead + EPS)
+    len_behind = jnp.sqrt(sq_behind + EPS)
+    raw_sq = (
+        sq_ahead / (len_ahead * len_ahead)
+        + sq_behind / (len_behind * len_behind)
+        + 2.0 * cross / (len_ahead * len_behind)
+    )
+    raw_len = jnp.sqrt(raw_sq + EPS)
+    tau_sq = raw_sq / (raw_sq + EPS)
+    chain_tab[ci] = pack(len_behind, len_ahead)
+    up, down = {}, {}
+
+    def lengths(step):
+        if step > 1:
+            up[step - 1].wait_recv()
+        if step <= chain_n // 2:
+            src = chain_tab.at[lax.rem(ci + chain_n + 1 - step, chain_n)]
+            up[step] = cp.group(src)
+            up[step].start(src, src, at_chain(1))
+        if 1 < step <= chain_n // 2:
+            down[step - 1].wait_recv()
+        if step < chain_n // 2:
+            src = chain_tab.at[lax.rem(ci + step - 1, chain_n)]
+            down[step] = cp.group(src)
+            down[step].start(src, src, at_chain(chain_n - 1))
+
+    lengths(1)
     back_resid(0)
     back_resid(1)
     rs_far_sum(2)
-    lengths(6)
+    lengths(2)
     grad(3, hid, dres)
     rs_start(3)
+    rs_near_start(0)
+    lengths(3)
     grad(4, hid, dres)
     rs_start(4)
+    rs_near_start(1)
+    lengths(4)
     back_pre(0)
     rs_far_sum(3)
-    lengths(7)
+    lengths(5)
+    rs_near_start(2)
     back_pre(1)
+    rs_far_sum(4)
+    lengths(6)
     grad(5, x, dpre)
     rs_start(5)
-    rs_far_sum(4)
-    lengths(8)
+    rs_near_sum(0)
+    rs_near_sum(1)
+    lengths(7)
     grad(6, x, dpre)
     rs_start(6)
-    rs_near_start(0)
-    rs_near_start(1)
+    rs_near_sum(2)
+    rs_end(0)
+    rs_end(1)
+    lengths(8)
     rs_far_sum(5)
-    rs_near_start(2)
+    rs_near_start(3)
     rs_far_sum(6)
-    rs_near_start(3)
     lengths(9)
     arc = jnp.zeros((1, 128), F32)
     band = jnp.zeros((1, 128), F32)
@@ -503,16 +507,11 @@
         arc = arc + jnp.where(j <= ci, length, 0.0)
         band = band + length
     band = band + chain_tab[chain_n - 1, 1:2]
-    rs_near_sum(0)
-    rs_near_sum(1)
     rs_near_start(4)
-    rs_near_sum(2)
     rs_near_start(5)
     rs_near_sum(3)
     rs_near_start(6)
     rs_near_sum(4)
-    rs_end(0)
-    rs_end(1)
     rs_end(2)
     rs_near_sum(5)
     rs_end(3)

time: 96.6 us -> 93.4 us (0.967)
  Pallas kernels: 95 us -> 91.3 us
    pallas_call x1, Pallas kernels: 93 us -> 89.3 us  [on_device(): pl.pallas_call(functools.partial(kernel, (chain_n, batch, classes)), out_...]
where the time goes in v4:
time: 93.4 us; the launch traced here: 92.8 us
  Pallas kernels  91.3 us (98%)
  between operations  1.45 us (2%)
    pallas_call x1, Pallas kernels, on_device(): pl.pallas_call(functools.partial(kernel, (chain_n, batch, classes)), out_...  89.3 us
    pallas_call x1, Pallas kernels, on_device(): pl.pallas_call(hand_out, out_shape=(jax.ShapeDtypeStruct(images_in.shape,...  2.03 us

profile of v4, /device:TPU:2, one launch (start us, length us, event | category | flops | bytes accessed | tf_op | source)
XLA Modules:
  0.0 92.8 jit_solution(15604599508377747464)
XLA Ops:
  1.3 89.3 %band_step.1 = (f32[64,1024]{1,0:T(8,128)}, f32[64,1024]{1,0:T(8,128)}, f32[64,1000]{1,0:T(8,128)}, f32[4,128]{1,0:T(4,128)}) custom-call(f32[1,64,1024]{2,1,0:T(8,128)} %im_in.1, f32[1,64,1024]{2,1,0:T(8,128)} %im_mid.1, f32[1,64,1000]{2,1,0:T(8,128)} %im_out.1, f32[2,64,1024]{2,1,0:T(8,128)} %en_in.1, f32[2,64,1024]{2,1,0:T(8,128)} %en_mid.1, ...), custom_call_target="tpu_custom_call" | custom-call | flops 18320719872 | bytes 10000000 | tf_op jit(solution)/shard_map/band_step/pallas_call | solution.py:622
  90.6 2.0 %hand_out.1 = (f32[1,64,1024]{2,1,0:T(8,128)}, f32[1,64,1024]{2,1,0:T(8,128)}, f32[1,64,1000]{2,1,0:T(8,128)}, f32[1]{0:T(128)}, f32[1]{0:T(128)}, /*index=5*/f32[1]{0:T(128)}) custom-call(f32[64,1024]{1,0:T(8,128)} %get-tuple-element.10.up_in, f32[64,1024]{1,0:T(8,128)} %get-tuple-element.11.up_mid, f32[64,1000]{1,0:T(8,128)} %get-tuple-element.12.up_out, ...), custom_call_target="tpu_custom_call" | custom-call | tf_op jit(solution)/shard_map/hand_out/pallas_call | solution.py:643

commit v5 on v4

--- a/solution.py
+++ b/solution.py
@@ -72,7 +72,7 @@
     W, G, RA1, RAd, RAs, R1, RB1, RBd, RBs, gsh,
     own_in, own_mid, own_out, nb_in, nb_mid, nb_out, e_in, e_mid, e_out, AH, BH,
     pool, onehot, rcol, lcol, x, hid, slope, resid, dlog, dres, dpre,
-    rows_ref, labs_ref, climb_ref, sums, chain_tab, out_in, out_mid, out_out, out_tab,
+    rows_ref, labs_ref, climb_ref, sums, chain_tab, out_tab,
     local_sem, send_sem, recv_sem,
 ):
     chain_n, batch, classes = dims
@@ -543,11 +543,10 @@
 
     out_tab[...] = pack(0.5 * norm * energy, arc / band, 0.5 * raw_len)
     save(out_tab, tab_ref)
-    for m, (up, dst) in enumerate(((out_in, up_in), (out_mid, up_mid), (out_out, up_out))):
+    for m, up in enumerate((up_in, up_mid, up_out)):
         n = up.shape[1]
         u = wa * AH[m, :, :n] + wb * BH[m, :, :n] - scale * gsh[m, :, :n]
         up[...] = own[m][...] + u
-        save(up, dst)
     for c in cp.all:
         c.wait_send()
     for c in saves:
@@ -611,9 +610,6 @@
         pltpu.SMEM((1,), jnp.int32),
         vm((2, SIDE * SIDE, 4, 128), F32),
         vm((chain_n, 4, 128), F32),
-        vm((shard, width), F32),
-        vm((shard, width), F32),
-        vm((shard, classes), F32),
         vm((4, 128), F32),
         pltpu.SemaphoreType.DMA((14,)),
         pltpu.SemaphoreType.DMA((N_COPIES,)),
@@ -622,16 +618,16 @@
     up_in, up_mid, up_out, tab = pl.pallas_call(
         functools.partial(kernel, (chain_n, batch, classes)),
         out_shape=(
-            jax.ShapeDtypeStruct((shard, hidden_units), F32),
-            jax.ShapeDtypeStruct((shard, width), F32),
-            jax.ShapeDtypeStruct((shard, classes), F32),
+            vm((shard, hidden_units), F32),
+            vm((shard, width), F32),
+            vm((shard, classes), F32),
             jax.ShapeDtypeStruct((4, 128), F32),
         ),
         in_specs=[any_spec] * 9 + [pl.BlockSpec(memory_space=pltpu.HBM)],
-        out_specs=(any_spec,) * 4,
+        out_specs=(vmem_spec,) * 3 + (any_spec,),
         scratch_shapes=scratch,
         compiler_params=pltpu.CompilerParams(
-            collective_id=0, has_side_effects=True, vmem_limit_bytes=56 * 2**20
+            collective_id=0, has_side_effects=True, vmem_limit_bytes=54 * 2**20
         ),
         cost_estimate=pl.CostEstimate(
             flops=2 * rows * width * (8 * width + pool_rows), bytes_accessed=10**7, transcendentals=10**6
@@ -653,7 +649,7 @@
         in_specs=[vmem_spec] * 3 + [smem_spec],
         out_specs=(vmem_spec,) * 3 + (smem_spec,) * 3,
         name="hand_out",
-    )(up_in, up_mid, up_out, tab)
+    )(*(pltpu.with_memory_space_constraint(up, pltpu.VMEM) for up in (up_in, up_mid, up_out)), tab)
 
 
 def solution(mesh):

time: 93.4 us -> 92.5 us (level)
  no operation moved by 1% of the time
where the time goes in v5:
time: 92.5 us; the launch traced here: 91.9 us
  Pallas kernels  90.5 us (98%)
  between operations  1.45 us (2%)
    pallas_call x1, Pallas kernels, on_device(): pl.pallas_call(functools.partial(kernel, (chain_n, batch, classes)), out_...  88.8 us

profile of v5, /device:TPU:2, one launch (start us, length us, event | category | flops | bytes accessed | tf_op | source)
XLA Modules:
  0.0 91.9 jit_solution(7180866416161874234)
XLA Ops:
  1.3 88.8 %band_step.1 = (f32[64,1024]{1,0:T(8,128)S(1)}, f32[64,1024]{1,0:T(8,128)S(1)}, f32[64,1000]{1,0:T(8,128)S(1)}, f32[4,128]{1,0:T(4,128)}) custom-call(f32[1,64,1024]{2,1,0:T(8,128)} %im_in.1, f32[1,64,1024]{2,1,0:T(8,128)} %im_mid.1, f32[1,64,1000]{2,1,0:T(8,128)} %im_out.1, f32[2,64,1024]{2,1,0:T(8,128)} %en_in.1, f32[2,64,1024]{2,1,0:T(8,128)} %en_mid.1, ...), custom_call_target="tpu_custom_call" | custom-call | flops 18320719872 | bytes 10000000 | tf_op jit(solution)/shard_map/band_step/pallas_call | solution.py:618
  90.1 1.6 %hand_out.1 = (f32[1,64,1024]{2,1,0:T(8,128)}, f32[1,64,1024]{2,1,0:T(8,128)}, f32[1,64,1000]{2,1,0:T(8,128)}, f32[1]{0:T(128)}, f32[1]{0:T(128)}, /*index=5*/f32[1]{0:T(128)}) custom-call(f32[64,1024]{1,0:T(8,128)S(1)} %get-tuple-element.10.up_in, f32[64,1024]{1,0:T(8,128)S(1)} %get-tuple-element.11.up_mid, f32[64,1000]{1,0:T(8,128)S(1)} %get-tuple-element.12.up_out, ...), custom_call_target="tpu_custom_call" | custom-call | tf_op jit(solution)/shard_map/hand_out/pallas_call | solution.py:639

commit v6 on v5

--- a/solution.py
+++ b/solution.py
@@ -329,10 +329,10 @@
             dlog[:, at : at + 128] = (err * norm).astype(BF16)
         return energy
 
+    ag_far_forward(1, SIDES)
+    ag_far_forward(1, ACROSS)
     ag_end(0)
     forward_in(0)
-    ag_far_forward(1, SIDES)
-    ag_far_forward(1, ACROSS)
     forward_in(1)
     ag_far_forward(2, SIDES)
     ag_far_forward(2, ACROSS)

time: 92.5 us -> 92.4 us (level)
  no operation moved by 1% of the time
where the time goes in v6:
time: 92.4 us; the launch traced here: 92 us
  Pallas kernels  90.6 us (98%)
  between operations  1.45 us (2%)
    pallas_call x1, Pallas kernels, on_device(): pl.pallas_call(functools.partial(kernel, (chain_n, batch, classes)), out_...  88.9 us

profile of v6, /device:TPU:2, one launch (start us, length us, event | category | flops | bytes accessed | tf_op | source)
XLA Modules:
  0.0 92.0 jit_solution(15258742932463727777)
XLA Ops:
  1.3 88.9 %band_step.1 = (f32[64,1024]{1,0:T(8,128)S(1)}, f32[64,1024]{1,0:T(8,128)S(1)}, f32[64,1000]{1,0:T(8,128)S(1)}, f32[4,128]{1,0:T(4,128)}) custom-call(f32[1,64,1024]{2,1,0:T(8,128)} %im_in.1, f32[1,64,1024]{2,1,0:T(8,128)} %im_mid.1, f32[1,64,1000]{2,1,0:T(8,128)} %im_out.1, f32[2,64,1024]{2,1,0:T(8,128)} %en_in.1, f32[2,64,1024]{2,1,0:T(8,128)} %en_mid.1, ...), custom_call_target="tpu_custom_call" | custom-call | flops 18320719872 | bytes 10000000 | tf_op jit(solution)/shard_map/band_step/pallas_call | solution.py:618
  90.2 1.6 %hand_out.1 = (f32[1,64,1024]{2,1,0:T(8,128)}, f32[1,64,1024]{2,1,0:T(8,128)}, f32[1,64,1000]{2,1,0:T(8,128)}, f32[1]{0:T(128)}, f32[1]{0:T(128)}, /*index=5*/f32[1]{0:T(128)}) custom-call(f32[64,1024]{1,0:T(8,128)S(1)} %get-tuple-element.10.up_in, f32[64,1024]{1,0:T(8,128)S(1)} %get-tuple-element.11.up_mid, f32[64,1000]{1,0:T(8,128)S(1)} %get-tuple-element.12.up_out, ...), custom_call_target="tpu_custom_call" | custom-call | tf_op jit(solution)/shard_map/hand_out/pallas_call | solution.py:639
